TPU v7x, 32 devices: a whole 2x2x4 slice. The times are simulated.
32 devices in a mesh: dp: 8 (over y, x, core), tensor: 4 (over z).
Axes of the slice: x: 2, y: 2, z: 4, core: 2. Of those that a mesh axis runs over, the one named last changes fastest.
Arguments:
- tokens: bfloat16 [4096, 2048], P(('dp', 'tensor')), may hold values from -6 to 6
- query_weight: bfloat16 [2048, 2048], P(None, 'tensor'), may hold values from -2 to 2
- key_weight: bfloat16 [2048, 2048], P(None, 'tensor'), may hold values from -2 to 2
- value_weight: bfloat16 [2048, 2048], P(None, 'tensor'), may hold values from -0.125 to 0.125
- query_gain: float32 [16, 128], P('tensor'), may hold values from 0.5 to 4.6
- key_gain: float32 [16, 128], P('tensor'), may hold values from 0.5 to 4.6
- out_weight: bfloat16 [2048, 2048], P('tensor'), may hold values from -0.125 to 0.125
- attn_gain: float32 [2048], replicated, may hold values from 0.5 to 1.5
- gate_weight: bfloat16 [2048, 8192], P(None, 'tensor'), may hold values from -0.125 to 0.125
- up_weight: bfloat16 [2048, 8192], P(None, 'tensor'), may hold values from -0.125 to 0.125
- down_weight: bfloat16 [8192, 2048], P('tensor'), may hold values from -0.0625 to 0.0625
- mlp_gain: float32 [2048], replicated, may hold values from 0.5 to 1.5
- cotangent: float32 [4096, 2048], P(('dp', 'tensor')), may hold values from -6 to 6
Outputs:
- output: float32 [4096, 2048], P(('dp', 'tensor'))
- input_grad: float32 [4096, 2048], P(('dp', 'tensor'))
- grad_query_weight: float32 [2048, 2048], P('dp', 'tensor')
- grad_key_weight: float32 [2048, 2048], P('dp', 'tensor')
- grad_value_weight: float32 [2048, 2048], P('dp', 'tensor')
- grad_query_gain: float32 [16, 128], P('tensor', 'dp')
- grad_key_gain: float32 [16, 128], P('tensor', 'dp')
- grad_out_weight: float32 [2048, 2048], P('tensor', 'dp')
- grad_attn_gain: float32 [2048], P(('dp', 'tensor'))
- grad_gate_weight: float32 [2048, 8192], P('dp', 'tensor')
- grad_up_weight: float32 [2048, 8192], P('dp', 'tensor')
- grad_down_weight: float32 [8192, 2048], P('tensor', 'dp')
- grad_mlp_gain: float32 [2048], P(('dp', 'tensor'))
All inputs are finite; a program needn't handle non-finite values.
Results may differ from a plain program's by a relative error of at most 0.018.
Values may be sent and summed in bfloat16 or wider, within the bound.
A program may use at most 256 MiB of HBM per device.

v0:
```python
import math

import jax
import jax.numpy as jnp
from jax import lax
from jax.sharding import PartitionSpec as P

L = 256


rms_eps = 1e-06
rope_base = 500000.0


def matmul(left, right):
    return jnp.dot(left, right, preferred_element_type=jnp.float32)


def matmul_nt(left, right):
    return lax.dot_general(
        left, right, (((1,), (1,)), ((), ())), preferred_element_type=jnp.float32
    )


def matmul_tn(left, right):
    return lax.dot_general(
        left, right, (((0,), (0,)), ((), ())), preferred_element_type=jnp.float32
    )


def rope_tables(row_total, half_dim):
    places = (jnp.arange(row_total, dtype=jnp.int32) % L).astype(jnp.float32)
    powers = jnp.arange(half_dim, dtype=jnp.int32).astype(jnp.float32) * (2.0 / (2 * half_dim))
    frequency = jnp.exp(-math.log(rope_base) * powers)
    angles = places[:, None] * frequency[None, :]
    return (jnp.cos(angles), jnp.sin(angles))


def rotate(values, cosine_table, sine_table):
    row_total = values.shape[0]
    half_dim = cosine_table.shape[1]
    halves = values.reshape(row_total, -1, 2, half_dim)
    first_half = halves[:, :, 0, :]
    second_half = halves[:, :, 1, :]
    cosine_b = cosine_table[:, None, :]
    sine_b = sine_table[:, None, :]
    turned = jnp.stack(
        [
            first_half * cosine_b - second_half * sine_b,
            second_half * cosine_b + first_half * sine_b,
        ],
        axis=2,
    )
    return turned.reshape(row_total, -1)


def rms_scale(values):
    return lax.rsqrt(jnp.mean(values * values, axis=-1, keepdims=True) + rms_eps)


def norm_back(values, scales, gain_row, upstream):
    weighted = upstream * gain_row
    inner_mean = jnp.mean(weighted * values, axis=-1, keepdims=True)
    return scales * (weighted - values * scales * scales * inner_mean)


def split_heads(array, head_count):
    return array.reshape(array.shape[0] // L, L, head_count, -1)


def causal_mask():
    position = jnp.arange(L, dtype=jnp.int32)
    return position[:, None] >= position[None, :]


def attend(query_rot, key_rot, value_proj, head_count):
    factor = 1.0 / math.sqrt(query_rot.shape[1] // head_count)
    scores = (
        jnp.einsum(
            "sqhd,skhd->shqk",
            split_heads(query_rot, head_count),
            split_heads(key_rot, head_count),
            preferred_element_type=jnp.float32,
        )
        * factor
    )
    masked = jnp.where(causal_mask(), scores, -jnp.inf)
    largest = jnp.max(masked, axis=-1, keepdims=True)
    expo_vals = jnp.exp(masked - largest)
    sum_exp = jnp.sum(expo_vals, axis=-1, keepdims=True)
    probability = (expo_vals / sum_exp).astype(jnp.bfloat16)
    mixed = jnp.einsum(
        "shqk,skhd->sqhd",
        probability,
        split_heads(value_proj, head_count),
        preferred_element_type=jnp.float32,
    )
    return (mixed.reshape(query_rot.shape[0], -1).astype(jnp.bfloat16), largest + jnp.log(sum_exp))


def attend_back(query_rot, key_rot, value_proj, logsum, grad_attended, head_count):
    factor = 1.0 / math.sqrt(query_rot.shape[1] // head_count)
    queries = split_heads(query_rot, head_count)
    keys_all = split_heads(key_rot, head_count)
    scores = (
        jnp.einsum("sqhd,skhd->shqk", queries, keys_all, preferred_element_type=jnp.float32)
        * factor
    )
    prob_full = jnp.exp(jnp.where(causal_mask(), scores - logsum, -jnp.inf))
    prob_low = prob_full.astype(jnp.bfloat16)
    grad_heads = split_heads(grad_attended, head_count)
    grad_value = jnp.einsum(
        "shqk,sqhd->skhd", prob_low, grad_heads, preferred_element_type=jnp.float32
    )
    grad_prob = jnp.einsum(
        "sqhd,skhd->shqk",
        grad_heads,
        split_heads(value_proj, head_count),
        preferred_element_type=jnp.float32,
    )
    row_dot = jnp.sum(prob_full * grad_prob, axis=-1, keepdims=True)
    grad_scores = (prob_full * (grad_prob - row_dot) * factor).astype(jnp.bfloat16)
    grad_query = jnp.einsum(
        "shqk,skhd->sqhd", grad_scores, keys_all, preferred_element_type=jnp.float32
    )
    grad_key = jnp.einsum(
        "shqk,sqhd->skhd", grad_scores, queries, preferred_element_type=jnp.float32
    )
    row_total = query_rot.shape[0]
    return (
        grad_query.reshape(row_total, -1),
        grad_key.reshape(row_total, -1),
        grad_value.reshape(row_total, -1).astype(jnp.bfloat16),
    )


def on_device(
    tokens,
    query_weight,
    key_weight,
    value_weight,
    query_gain,
    key_gain,
    out_weight,
    attn_gain,
    gate_weight,
    up_weight,
    down_weight,
    mlp_gain,
    cotangent,
):
    model_width = tokens.shape[1]
    head_count = query_gain.shape[0]
    query_flat = query_gain.reshape(-1)
    key_flat = key_gain.reshape(-1)
    gathered = lax.all_gather(tokens, "tensor", axis=0, tiled=True)
    row_total = gathered.shape[0]
    cosine_table, sine_table = rope_tables(row_total, query_gain.shape[1] // 2)
    query_proj = matmul(gathered, query_weight)
    key_proj = matmul(gathered, key_weight)
    value_proj = matmul(gathered, value_weight).astype(jnp.bfloat16)
    query_square, key_square = lax.psum(
        (jnp.sum(query_proj * query_proj, axis=-1), jnp.sum(key_proj * key_proj, axis=-1)), "tensor"
    )
    query_scale = lax.rsqrt(query_square / model_width + rms_eps)[:, None]
    key_scale = lax.rsqrt(key_square / model_width + rms_eps)[:, None]
    query_rot = rotate(query_proj * query_scale * query_flat, cosine_table, sine_table).astype(
        jnp.bfloat16
    )
    key_rot = rotate(key_proj * key_scale * key_flat, cosine_table, sine_table).astype(jnp.bfloat16)
    attended, logsum = attend(query_rot, key_rot, value_proj, head_count)
    attn_branch = lax.psum_scatter(
        matmul(attended, out_weight), "tensor", scatter_dimension=0, tiled=True
    )
    attn_scale = rms_scale(attn_branch)
    hidden = tokens.astype(jnp.float32) + attn_branch * attn_scale * attn_gain
    hidden_rows = lax.all_gather(hidden.astype(jnp.bfloat16), "tensor", axis=0, tiled=True)
    gate_proj = matmul(hidden_rows, gate_weight)
    up_proj = matmul(hidden_rows, up_weight)
    sigmoid_gate = jax.nn.sigmoid(gate_proj)
    swish_gate = gate_proj * sigmoid_gate
    activation = (swish_gate * up_proj).astype(jnp.bfloat16)
    mlp_branch = lax.psum_scatter(
        matmul(activation, down_weight), "tensor", scatter_dimension=0, tiled=True
    )
    mlp_scale = rms_scale(mlp_branch)
    output = hidden + mlp_branch * mlp_scale * mlp_gain
    part_mlp_gain = jnp.sum(cotangent * mlp_branch * mlp_scale, axis=0)
    grad_mlp = norm_back(mlp_branch, mlp_scale, mlp_gain, cotangent).astype(jnp.bfloat16)
    grad_mlp_rows = lax.all_gather(grad_mlp, "tensor", axis=0, tiled=True)
    grad_act = matmul_nt(grad_mlp_rows, down_weight)
    grad_gate = (
        grad_act * up_proj * sigmoid_gate * (1.0 + gate_proj * (1.0 - sigmoid_gate))
    ).astype(jnp.bfloat16)
    grad_up = (grad_act * swish_gate).astype(jnp.bfloat16)
    term_down = matmul_tn(activation, grad_mlp_rows)
    term_gate = matmul_tn(hidden_rows, grad_gate)
    term_up = matmul_tn(hidden_rows, grad_up)
    grad_hidden = cotangent + lax.psum_scatter(
        matmul_nt(grad_gate, gate_weight) + matmul_nt(grad_up, up_weight),
        "tensor",
        scatter_dimension=0,
        tiled=True,
    )
    part_attn_gain = jnp.sum(grad_hidden * attn_branch * attn_scale, axis=0)
    grad_branch = norm_back(attn_branch, attn_scale, attn_gain, grad_hidden).astype(jnp.bfloat16)
    grad_branch_rows = lax.all_gather(grad_branch, "tensor", axis=0, tiled=True)
    grad_attended = matmul_nt(grad_branch_rows, out_weight).astype(jnp.bfloat16)
    term_out = matmul_tn(attended, grad_branch_rows)
    grad_query_rot, grad_key_rot, grad_value = attend_back(
        query_rot, key_rot, value_proj, logsum, grad_attended, head_count
    )
    grad_query_normed = rotate(grad_query_rot, cosine_table, -sine_table)
    grad_key_normed = rotate(grad_key_rot, cosine_table, -sine_table)
    term_query_gain = jnp.sum(grad_query_normed * query_proj * query_scale, axis=0).reshape(
        query_gain.shape
    )
    term_key_gain = jnp.sum(grad_key_normed * key_proj * key_scale, axis=0).reshape(key_gain.shape)
    query_weighted = grad_query_normed * query_flat
    key_weighted = grad_key_normed * key_flat
    query_inner, key_inner = lax.psum(
        (jnp.sum(query_weighted * query_proj, axis=-1), jnp.sum(key_weighted * key_proj, axis=-1)),
        "tensor",
    )
    grad_query = (
        query_scale
        * (
            query_weighted
            - query_proj * query_scale * query_scale * (query_inner / model_width)[:, None]
        )
    ).astype(jnp.bfloat16)
    grad_key = (
        key_scale
        * (key_weighted - key_proj * key_scale * key_scale * (key_inner / model_width)[:, None])
    ).astype(jnp.bfloat16)
    term_query = matmul_tn(gathered, grad_query)
    term_key = matmul_tn(gathered, grad_key)
    term_value = matmul_tn(gathered, grad_value)
    input_grad = grad_hidden + lax.psum_scatter(
        (
            matmul_nt(grad_query, query_weight)
            + matmul_nt(grad_key, key_weight)
            + matmul_nt(grad_value, value_weight)
        ).astype(jnp.bfloat16),
        "tensor",
        scatter_dimension=0,
        tiled=True,
    ).astype(jnp.float32)
    summed_attn_gain, summed_mlp_gain = (
        lax.psum_scatter(part_attn_gain, ("dp", "tensor"), scatter_dimension=0, tiled=True),
        lax.psum_scatter(part_mlp_gain, ("dp", "tensor"), scatter_dimension=0, tiled=True),
    )
    (
        summed_query,
        summed_key,
        summed_value,
        summed_out,
        summed_query_gain,
        summed_key_gain,
        summed_gate,
        summed_up,
        summed_down,
    ) = (
        lax.psum_scatter(term_query, "dp", scatter_dimension=0, tiled=True),
        lax.psum_scatter(term_key, "dp", scatter_dimension=0, tiled=True),
        lax.psum_scatter(term_value, "dp", scatter_dimension=0, tiled=True),
        lax.psum_scatter(term_out, "dp", scatter_dimension=1, tiled=True),
        lax.psum_scatter(term_query_gain, "dp", scatter_dimension=1, tiled=True),
        lax.psum_scatter(term_key_gain, "dp", scatter_dimension=1, tiled=True),
        lax.psum_scatter(term_gate, "dp", scatter_dimension=0, tiled=True),
        lax.psum_scatter(term_up, "dp", scatter_dimension=0, tiled=True),
        lax.psum_scatter(term_down, "dp", scatter_dimension=1, tiled=True),
    )
    return (
        output,
        input_grad,
        summed_query,
        summed_key,
        summed_value,
        summed_query_gain,
        summed_key_gain,
        summed_out,
        summed_attn_gain,
        summed_gate,
        summed_up,
        summed_down,
        summed_mlp_gain,
    )


def solution(mesh):
    placed = (
        P(("dp", "tensor"), None),
        P(None, "tensor"),
        P(None, "tensor"),
        P(None, "tensor"),
        P("tensor", None),
        P("tensor", None),
        P("tensor", None),
        P(),
        P(None, "tensor"),
        P(None, "tensor"),
        P("tensor", None),
        P(),
        P(("dp", "tensor"), None),
    )
    return jax.shard_map(
        on_device,
        mesh=mesh,
        in_specs=placed,
        out_specs=(
            P(("dp", "tensor"), None),
            P(("dp", "tensor"), None),
            P("dp", "tensor"),
            P("dp", "tensor"),
            P("dp", "tensor"),
            P("tensor", "dp"),
            P("tensor", "dp"),
            P("tensor", "dp"),
            P(("dp", "tensor")),
            P("dp", "tensor"),
            P("dp", "tensor"),
            P("tensor", "dp"),
            P(("dp", "tensor")),
        ),
        check_vma=False,
    )
```

profile of v0, /device:TPU:0, one launch (start us, length us, event | category | flops | bytes accessed | tf_op | source)
XLA Modules:
  0.0 1262.9 jit_solution(16068228856149152544)
XLA Ops:
  9.2 48.8 %all-gather.5.cloned.1.call-done = bf16[512,2048]{1,0:T(8,128)(2,1)} async-done(((bf16[128,2048]{1,0:T(8,128)(2,1)}), bf16[512,2048]{1,0:T(8,128)(2,1)}) %all-gather.5.cloned.1.call-update) | async-done | bytes 2097168 | tf_op jit(solution)/shard_map/all_gather | solution.py:156
  58.0 3.5 convolution_convert_fusion.1
  62.4 3.0 multiply_reduce_fusion.9
  65.5 2.3 multiply_reduce_fusion.10
  67.7 10.4 all-reduce.4
  87.1 5.0 fusion.33
  92.2 75.1 %reduce-scatter.18.cloned.1.call-done = f32[128,2048]{1,0:T(8,128)} async-done(((f32[512,2048]{1,0:T(8,128)}), f32[128,2048]{1,0:T(8,128)}) %reduce-scatter.18.cloned.1.call-update) | async-done | bytes 1048592 | tf_op jit(solution)/shard_map/reduce_scatter | solution.py:172
  168.7 2.2 fusion.28
  171.5 45.8 %all-gather.7.cloned.1.call-done = bf16[512,2048]{1,0:T(8,128)(2,1)} async-done(((bf16[128,2048]{1,0:T(8,128)(2,1)}), bf16[512,2048]{1,0:T(8,128)(2,1)}) %all-gather.7.cloned.1.call-update) | async-done | bytes 2097168 | tf_op jit(solution)/shard_map/all_gather | solution.py:177
  217.3 8.5 fusion.66
  225.9 11.7 multiply_convert_fusion.2
  238.9 6.2 fusion.67
  245.2 75.7 %reduce-scatter.20.cloned.1.call-done = f32[128,2048]{1,0:T(8,128)} async-done(((f32[512,2048]{1,0:T(8,128)}), f32[128,2048]{1,0:T(8,128)}) %reduce-scatter.20.cloned.1.call-update) | async-done | bytes 1048592 | tf_op jit(solution)/shard_map/reduce_scatter | solution.py:183
  325.2 46.1 %all-gather.9.cloned.1.call-done = bf16[512,2048]{1,0:T(8,128)(2,1)} async-done(((bf16[128,2048]{1,0:T(8,128)(2,1)}), bf16[512,2048]{1,0:T(8,128)(2,1)}) %all-gather.9.cloned.1.call-update) | async-done | bytes 2097168 | tf_op jit(solution)/shard_map/all_gather | solution.py:190
  371.3 11.9 multiply_convert_fusion
  383.3 8.5 fusion.68
  391.8 9.5 convolution_add_fusion
  401.4 75.7 %reduce-scatter.22.cloned.1.call-done = f32[128,2048]{1,0:T(8,128)} async-done(((f32[512,2048]{1,0:T(8,128)}), f32[128,2048]{1,0:T(8,128)}) %reduce-scatter.22.cloned.1.call-update) | async-done | bytes 1048592 | tf_op jit(solution)/shard_map/reduce_scatter | solution.py:199
  480.9 46.1 %all-gather.11.cloned.1.call-done = bf16[512,2048]{1,0:T(8,128)(2,1)} async-done(((bf16[128,2048]{1,0:T(8,128)(2,1)}), bf16[512,2048]{1,0:T(8,128)(2,1)}) %all-gather.11.cloned.1.call-update) | async-done | bytes 2097168 | tf_op jit(solution)/shard_map/all_gather | solution.py:207
  527.0 4.3 convolution_convert_fusion
  533.6 2.8 fusion.45
  536.4 5.8 fusion.12
  542.3 5.0 fusion.15
  549.1 2.1 reshape_reshape.7
  551.2 3.0 copy.67
  554.2 3.0 reshape_reshape.6
  557.2 2.4 multiply_subtract_fusion
  564.9 10.1 all-reduce.3
  577.2 3.3 fusion.70
  580.5 3.3 fusion.69
  585.6 6.7 add_convert_fusion
  593.4 4.8 convolution_bitcast_fusion.1
  599.2 4.9 convolution_bitcast_fusion.2
  604.2 4.8 convolution_bitcast_fusion
  610.1 4.8 fusion.31
  615.2 12.5 fusion.73
  627.8 12.7 %fusion.72 = f32[2048,2048]{1,0:T(8,128)} fusion(bf16[512,2048]{1,0:T(8,128)(2,1)} %all-gather.7.cloned.1.call-done, bf16[512,2048]{1,0:T(8,128)(2,1)} %copy-done.40), kind=kOutput, calls=%fused_computation.127 | convolution fusion | flops 4294967296 | bytes 20971520 | tf_op jit(solution)/shard_map/dot_general | solution.py:26
  640.8 12.5 fusion.71
  653.4 41.2 %all-reduce.2 = (f32[2048]{0:T(1024)S(1)}, f32[2048]{0:T(1024)S(1)}) all-reduce(f32[2048]{0:T(1024)S(1)} %get-tuple-element.54, f32[2048]{0:T(1024)S(1)} %get-tuple-element.52), channel_id=12, replica_groups=mesh['dp'=8,'tensor'=4] {'dp','tensor'}, use_global_device_ids=true, to_apply=%region_28.29.clone | all-reduce | flops 4096 | bytes 32768
  698.4 2.1 convert_add_fusion
  700.5 31.6 %reduce-scatter.28.cloned.1.call-done = f32[256,512]{0,1:T(8,128)} async-done(((f32[2048,512]{0,1:T(8,128)}), f32[256,512]{0,1:T(8,128)}) %reduce-scatter.28.cloned.1.call-update) | async-done | bytes 524304 | tf_op jit(solution)/shard_map/reduce_scatter | solution.py:265
  732.1 2.0 copy.75
  734.1 52.3 %reduce-scatter.26.cloned.1.call-done = f32[256,512]{0,1:T(8,128)} async-done(((f32[2048,512]{0,1:T(8,128)}), f32[256,512]{0,1:T(8,128)}) %reduce-scatter.26.cloned.1.call-update) | async-done | bytes 524304 | tf_op jit(solution)/shard_map/reduce_scatter | solution.py:264
  788.5 52.4 %reduce-scatter.30.cloned.1.call-done = f32[256,512]{0,1:T(8,128)} async-done(((f32[2048,512]{0,1:T(8,128)}), f32[256,512]{0,1:T(8,128)}) %reduce-scatter.30.cloned.1.call-update) | async-done | bytes 524304 | tf_op jit(solution)/shard_map/reduce_scatter | solution.py:266
  842.9 52.8 %reduce-scatter.32.cloned.1.call-done = f32[512,256]{1,0:T(8,128)} async-done(((f32[512,2048]{1,0:T(8,128)}), f32[512,256]{1,0:T(8,128)}) %reduce-scatter.32.cloned.1.call-update) | async-done | bytes 524304 | tf_op jit(solution)/shard_map/reduce_scatter | solution.py:267
  895.8 120.0 %reduce-scatter.38.cloned.1.call-done = f32[2048,256]{1,0:T(8,128)} async-done(((f32[2048,2048]{1,0:T(8,128)}), f32[2048,256]{1,0:T(8,128)}) %reduce-scatter.38.cloned.1.call-update) | async-done | bytes 2097168 | tf_op jit(solution)/shard_map/reduce_scatter | solution.py:272
  1015.7 120.2 %reduce-scatter.36.cloned.1.call-done = f32[256,2048]{1,0:T(8,128)} async-done(((f32[2048,2048]{1,0:T(8,128)}), f32[256,2048]{1,0:T(8,128)}) %reduce-scatter.36.cloned.1.call-update) | async-done | bytes 2097168 | tf_op jit(solution)/shard_map/reduce_scatter | solution.py:271
  1136.0 120.2 %reduce-scatter.34.cloned.1.call-done = f32[256,2048]{1,0:T(8,128)} async-done(((f32[2048,2048]{1,0:T(8,128)}), f32[256,2048]{1,0:T(8,128)}) %reduce-scatter.34.cloned.1.call-update) | async-done | bytes 2097168 | tf_op jit(solution)/shard_map/reduce_scatter | solution.py:270
  (175 shorter events, 48.3 us)
Async XLA Ops:
  7.2 55.2 %copy-start = (bf16[2048,512]{1,0:T(8,128)(2,1)S(1)}, bf16[2048,512]{1,0:T(8,128)(2,1)}, u32[]{:S(2)}) copy-start(bf16[2048,512]{1,0:T(8,128)(2,1)} %param.15) | copy-start | bytes 6291460
  7.2 50.8 %all-gather.5.cloned.1.call-start = ((), (), s32[]{:S(2)}) async-start(), calls=%async_computation.13 | async-start | bytes 2621440 | tf_op jit(solution)/shard_map/all_gather | solution.py:156
  7.9 159.4 %reduce-scatter.18.cloned.1.call-start = ((), (), s32[]{:S(2)}) async-start(), calls=%async_computation.14 | async-start | bytes 5242880 | tf_op jit(solution)/shard_map/reduce_scatter | solution.py:172
  62.4 3.1 copy-start.1
  62.4 3.1 copy-start.28
  65.4 13.5 %copy-start.8 = (f32[512,512]{0,1:T(8,128)}, f32[512,512]{0,1:T(8,128)S(1)}, u32[]{:S(2)}) copy-start(f32[512,512]{0,1:T(8,128)S(1)} %get-tuple-element.89) | copy-start | bytes 3145732
  65.5 13.5 %copy-start.36 = (f32[4,128]{1,0:T(4,128)S(1)}, f32[4,128]{1,0:T(4,128)}, u32[]{:S(2)}) copy-start(f32[4,128]{1,0:T(4,128)} %param.18) | copy-start | bytes 6148
  67.7 11.4 copy-start.35
  81.1 2.3 copy-start.31
  81.1 3.1 copy-start.25
  87.1 5.0 copy-start.21
  92.1 76.6 %copy-start.19 = (bf16[128,2048]{1,0:T(8,128)(2,1)S(1)}, bf16[128,2048]{1,0:T(8,128)(2,1)}, u32[]{:S(2)}) copy-start(bf16[128,2048]{1,0:T(8,128)(2,1)} %param.13) | copy-start | bytes 1572868
  92.1 76.6 %copy-start.33 = (f32[2048]{0:T(1024)S(1)}, f32[2048]{0:T(1024)}, u32[]{:S(2)}) copy-start(f32[2048]{0:T(1024)} %param.20) | copy-start | bytes 24580
  92.1 125.2 %all-gather.7.cloned.1.call-start = ((), (), s32[]{:S(2)}) async-start(), calls=%async_computation.15 | async-start | bytes 2621440 | tf_op jit(solution)/shard_map/all_gather | solution.py:177
  171.0 149.9 %reduce-scatter.20.cloned.1.call-start = ((), (), s32[]{:S(2)}) async-start(), calls=%async_computation.16 | async-start | bytes 5242880 | tf_op jit(solution)/shard_map/reduce_scatter | solution.py:183
  217.3 8.5 copy-start.37
  217.3 21.6 %slice-start = ((s8[8388608]{0:T(1024)(128)(4,1)}), s8[4194304]{0:T(1024)(128)(4,1)S(1)}, s32[]{:S(2)}) async-start(s8[8388608]{0:T(1024)(128)(4,1)} %bitcast.138), calls=%async_computation.30 | async-start | bytes 8388608
  225.9 11.7 copy-start.41
  225.9 13.0 %slice-start.1 = ((s8[8388608]{0:T(1024)(128)(4,1)}), s8[4194304]{0:T(1024)(128)(4,1)S(1)}, s32[]{:S(2)}) async-start(s8[8388608]{0:T(1024)(128)(4,1)} %bitcast.138), calls=%async_computation.31 | async-start | bytes 8388608
  245.1 77.3 %copy-start.5 = (f32[128,2048]{1,0:T(8,128)S(1)}, f32[128,2048]{1,0:T(8,128)}, u32[]{:S(2)}) copy-start(f32[128,2048]{1,0:T(8,128)} %param.25) | copy-start | bytes 3145732
  245.1 77.3 %copy-start.34 = (f32[2048]{0:T(1024)S(1)}, f32[2048]{0:T(1024)}, u32[]{:S(2)}) copy-start(f32[2048]{0:T(1024)} %param.24) | copy-start | bytes 24580
  245.1 126.2 %all-gather.9.cloned.1.call-start = ((), (), s32[]{:S(2)}) async-start(), calls=%async_computation.17 | async-start | bytes 2621440 | tf_op jit(solution)/shard_map/all_gather | solution.py:190
  320.9 3.0 copy-start.3
  325.0 152.1 %reduce-scatter.22.cloned.1.call-start = ((), (), s32[]{:S(2)}) async-start(), calls=%async_computation.18 | async-start | bytes 5242880 | tf_op jit(solution)/shard_map/reduce_scatter | solution.py:199
  383.3 8.5 copy-start.39
  383.3 8.5 copy-start.40
  401.3 75.8 %copy-start.2 = (f32[128,2048]{1,0:T(8,128)S(1)}, f32[128,2048]{1,0:T(8,128)}, u32[]{:S(2)}) copy-start(f32[128,2048]{1,0:T(8,128)} %reduce-scatter.18.cloned.1.call-done) | copy-start | bytes 3145732
  401.3 125.7 %all-gather.11.cloned.1.call-start = ((), (), s32[]{:S(2)}) async-start(), calls=%async_computation.19 | async-start | bytes 2621440 | tf_op jit(solution)/shard_map/all_gather | solution.py:207
  477.1 2.0 copy-start.4
  477.1 2.0 copy-start.20
  480.7 215.0 %reduce-scatter.42.cloned.1.call-start = ((), (), s32[]{:S(2)}) async-start(), calls=%async_computation.29 | async-start | bytes 73728
  531.3 2.3 copy-start.26
  533.6 2.8 copy-start.30
  562.3 134.7 %reduce-scatter.40.cloned.1.call-start = ((), (), s32[]{:S(2)}) async-start(), calls=%async_computation.28 | async-start | bytes 73728
  576.9 3.6 copy-start.15
  577.2 3.3 copy-start.17
  577.2 3.3 copy-start.29
  580.5 3.3 copy-start.24
  580.5 3.3 copy-start.27
  585.5 112.9 %reduce-scatter.24.cloned.1.call-start = ((), (), s32[]{:S(2)}) async-start(), calls=%async_computation.20 | async-start | bytes 2621440 | tf_op jit(solution)/shard_map/reduce_scatter | solution.py:239
  592.3 139.8 %reduce-scatter.28.cloned.1.call-start = ((), (), s32[]{:S(2)}) async-start(), calls=%async_computation.22 | async-start | bytes 4718592 | tf_op jit(solution)/shard_map/reduce_scatter | solution.py:265
  598.2 188.2 %reduce-scatter.26.cloned.1.call-start = ((), (), s32[]{:S(2)}) async-start(), calls=%async_computation.21 | async-start | bytes 4718592 | tf_op jit(solution)/shard_map/reduce_scatter | solution.py:264
  604.2 236.7 %reduce-scatter.30.cloned.1.call-start = ((), (), s32[]{:S(2)}) async-start(), calls=%async_computation.23 | async-start | bytes 4718592 | tf_op jit(solution)/shard_map/reduce_scatter | solution.py:266
  609.1 286.7 %reduce-scatter.32.cloned.1.call-start = ((), (), s32[]{:S(2)}) async-start(), calls=%async_computation.24 | async-start | bytes 4718592 | tf_op jit(solution)/shard_map/reduce_scatter | solution.py:267
  615.0 400.8 %reduce-scatter.38.cloned.1.call-start = ((), (), s32[]{:S(2)}) async-start(), calls=%async_computation.27 | async-start | bytes 18874368 | tf_op jit(solution)/shard_map/reduce_scatter | solution.py:272
  627.7 508.2 %reduce-scatter.36.cloned.1.call-start = ((), (), s32[]{:S(2)}) async-start(), calls=%async_computation.26 | async-start | bytes 18874368 | tf_op jit(solution)/shard_map/reduce_scatter | solution.py:271
  640.5 615.6 %reduce-scatter.34.cloned.1.call-start = ((), (), s32[]{:S(2)}) async-start(), calls=%async_computation.25 | async-start | bytes 18874368 | tf_op jit(solution)/shard_map/reduce_scatter | solution.py:270
  653.3 45.1 %copy-start.7 = (f32[128,2048]{1,0:T(8,128)S(1)}, f32[128,2048]{1,0:T(8,128)}, u32[]{:S(2)}) copy-start(f32[128,2048]{1,0:T(8,128)} %copy-done.6) | copy-start | bytes 3145732
  (13 other events, 16.8 us)
Sparse Core Ops, SparseCore 0:
  9.6 48.3 all-gather.4
  92.3 74.9 reduce-scatter.17
  171.1 46.1 all-gather.6
  245.2 75.5 reduce-scatter.19
  325.1 46.1 all-gather.8
  401.5 75.5 reduce-scatter.21
  480.8 46.1 all-gather.10
  562.5 32.2 reduce-scatter.41
  598.4 33.5 reduce-scatter.39
  634.1 44.0 reduce-scatter.23
  681.5 50.5 reduce-scatter.27
  735.3 51.0 reduce-scatter.25
  789.8 51.0 reduce-scatter.29
  844.7 51.0 reduce-scatter.31
  899.7 115.9 reduce-scatter.37
  1019.7 116.1 reduce-scatter.35
  1139.9 116.1 reduce-scatter.33
where the time goes:
time: 1270 us; the launch traced here: 1260 us
  waiting for transfers between devices  964 us (76%)
  matrix products  163 us (13%)
  blocking collectives  61.7 us (5%)
  local copies, waits for them, and re-layouts  35 us (3%)
  other arithmetic  23.3 us (2%)
  between operations  14.7 us (1%)
    reduce_scatter x1, waiting for transfers between devices, on_device(): lax.psum_scatter(term_up, 'dp', scatter_dimension=0, tiled=True)  120 us
    reduce_scatter x1, waiting for transfers between devices, on_device(): lax.psum_scatter(term_gate, 'dp', scatter_dimension=0, tiled=True)  120 us
    reduce_scatter x1, waiting for transfers between devices, on_device(): lax.psum_scatter(term_down, 'dp', scatter_dimension=1, tiled=True)  120 us
    reduce_scatter x1, waiting for transfers between devices, on_device(): lax.psum_scatter(matmul(activation, down_weight), 'tensor', scatter_dimen...  75.7 us
    reduce_scatter x1, waiting for transfers between devices, on_device(): lax.psum_scatter(matmul_nt(grad_gate, gate_weight) + matmul_nt(grad_up, u...  75.7 us
    reduce_scatter x1, waiting for transfers between devices, on_device(): lax.psum_scatter(matmul(attended, out_weight), 'tensor', scatter_dimensio...  75.1 us
    dot_general x7, matrix products, matmul_tn(): lax.dot_general(left, right, (((0,), (0,)), ((), ())), preferred_element_...  57.2 us
    reduce_scatter x1, waiting for transfers between devices, on_device(): lax.psum_scatter(term_out, 'dp', scatter_dimension=1, tiled=True)  52.8 us
  transfers between devices with their start and end apart: 17, of which 14 were waited for; matrix products, arithmetic and copies ran while one was open for 7% of the time, Pallas kernels for 0%

commit v1 on v0

--- a/solution.py
+++ b/solution.py
@@ -1,3 +1,4 @@
+import functools
 import math
 
 import jax
@@ -134,7 +135,84 @@
     )
 
 
+def swap_pairs(size, step):
+    return [(place, place ^ step) for place in range(size)]
+
+
+def owner_order(bits):
+    if not bits:
+        return [0]
+    rest = owner_order(bits[1:])
+    return [member | (1 << bits[0]) for member in rest] + rest
+
+
+def half_plans(size):
+    bits = list(range(1, size.bit_length() - 1))
+    return bits, bits[1:] + bits[:1]
+
+
+def by_owner(columns, size):
+    me = lax.axis_index("dp")
+    width = columns.shape[1] // size
+    part = width // 2
+    sent, kept = [], []
+    for half, bits in enumerate(half_plans(size)):
+        for mask in owner_order(bits):
+            for flip, held in ((1, sent), (0, kept)):
+                start = (me ^ (mask | flip)) * width + half * part
+                held.append(lax.dynamic_slice_in_dim(columns, start, part, axis=1))
+    return jnp.concatenate(sent, axis=1), jnp.concatenate(kept, axis=1)
+
+
+def exchange(values, size, step):
+    return lax.ppermute(values, "dp", swap_pairs(size, step))
+
+
+def halve(values, axis, size, bits):
+    for bit in bits:
+        cut = values.shape[axis] // 2
+        sent = lax.slice_in_dim(values, 0, cut, axis=axis).astype(jnp.bfloat16)
+        arrived = exchange(sent, size, 1 << bit)
+        values = lax.slice_in_dim(values, cut, 2 * cut, axis=axis) + arrived.astype(jnp.float32)
+    return values
+
+
+def reduce_product(product, sent, kept, axis, size):
+    arrived = exchange(product(sent).astype(jnp.bfloat16), size, 1)
+    held = product(kept) + arrived.astype(jnp.float32)
+    cut = held.shape[axis] // 2
+    first, second = half_plans(size)
+    return jnp.concatenate(
+        [
+            halve(lax.slice_in_dim(held, 0, cut, axis=axis), axis, size, first),
+            halve(lax.slice_in_dim(held, cut, 2 * cut, axis=axis), axis, size, second),
+        ],
+        axis=axis,
+    )
+
+
+def add_all(values, name, size):
+    step = 1
+    while step < size:
+        values = values + lax.ppermute(values, name, swap_pairs(size, step))
+        step *= 2
+    return values
+
+
+def own_part(values, axis, place, count):
+    part = values.shape[axis] // count
+    return lax.dynamic_slice_in_dim(values, place * part, part, axis=axis)
+
+
+def scatter_low(values):
+    return lax.psum_scatter(
+        values.astype(jnp.bfloat16), "tensor", scatter_dimension=0, tiled=True
+    ).astype(jnp.float32)
+
+
 def on_device(
+    dp_size,
+    tensor_size,
     tokens,
     query_weight,
     key_weight,
@@ -169,9 +247,7 @@
     )
     key_rot = rotate(key_proj * key_scale * key_flat, cosine_table, sine_table).astype(jnp.bfloat16)
     attended, logsum = attend(query_rot, key_rot, value_proj, head_count)
-    attn_branch = lax.psum_scatter(
-        matmul(attended, out_weight), "tensor", scatter_dimension=0, tiled=True
-    )
+    attn_branch = scatter_low(matmul(attended, out_weight))
     attn_scale = rms_scale(attn_branch)
     hidden = tokens.astype(jnp.float32) + attn_branch * attn_scale * attn_gain
     hidden_rows = lax.all_gather(hidden.astype(jnp.bfloat16), "tensor", axis=0, tiled=True)
@@ -180,9 +256,7 @@
     sigmoid_gate = jax.nn.sigmoid(gate_proj)
     swish_gate = gate_proj * sigmoid_gate
     activation = (swish_gate * up_proj).astype(jnp.bfloat16)
-    mlp_branch = lax.psum_scatter(
-        matmul(activation, down_weight), "tensor", scatter_dimension=0, tiled=True
-    )
+    mlp_branch = scatter_low(matmul(activation, down_weight))
     mlp_scale = rms_scale(mlp_branch)
     output = hidden + mlp_branch * mlp_scale * mlp_gain
     part_mlp_gain = jnp.sum(cotangent * mlp_branch * mlp_scale, axis=0)
@@ -193,20 +267,24 @@
         grad_act * up_proj * sigmoid_gate * (1.0 + gate_proj * (1.0 - sigmoid_gate))
     ).astype(jnp.bfloat16)
     grad_up = (grad_act * swish_gate).astype(jnp.bfloat16)
-    term_down = matmul_tn(activation, grad_mlp_rows)
-    term_gate = matmul_tn(hidden_rows, grad_gate)
-    term_up = matmul_tn(hidden_rows, grad_up)
-    grad_hidden = cotangent + lax.psum_scatter(
-        matmul_nt(grad_gate, gate_weight) + matmul_nt(grad_up, up_weight),
-        "tensor",
-        scatter_dimension=0,
-        tiled=True,
+    summed_down = reduce_product(
+        lambda part: matmul_tn(activation, part), *by_owner(grad_mlp_rows, dp_size), 1, dp_size
+    )
+    hidden_parts = by_owner(hidden_rows, dp_size)
+    summed_gate = reduce_product(
+        lambda part: matmul_tn(part, grad_gate), *hidden_parts, 0, dp_size
+    )
+    summed_up = reduce_product(lambda part: matmul_tn(part, grad_up), *hidden_parts, 0, dp_size)
+    grad_hidden = cotangent + scatter_low(
+        matmul_nt(grad_gate, gate_weight) + matmul_nt(grad_up, up_weight)
     )
     part_attn_gain = jnp.sum(grad_hidden * attn_branch * attn_scale, axis=0)
     grad_branch = norm_back(attn_branch, attn_scale, attn_gain, grad_hidden).astype(jnp.bfloat16)
     grad_branch_rows = lax.all_gather(grad_branch, "tensor", axis=0, tiled=True)
     grad_attended = matmul_nt(grad_branch_rows, out_weight).astype(jnp.bfloat16)
-    term_out = matmul_tn(attended, grad_branch_rows)
+    summed_out = reduce_product(
+        lambda part: matmul_tn(attended, part), *by_owner(grad_branch_rows, dp_size), 1, dp_size
+    )
     grad_query_rot, grad_key_rot, grad_value = attend_back(
         query_rot, key_rot, value_proj, logsum, grad_attended, head_count
     )
@@ -233,44 +311,37 @@
         key_scale
         * (key_weighted - key_proj * key_scale * key_scale * (key_inner / model_width)[:, None])
     ).astype(jnp.bfloat16)
-    term_query = matmul_tn(gathered, grad_query)
-    term_key = matmul_tn(gathered, grad_key)
-    term_value = matmul_tn(gathered, grad_value)
-    input_grad = grad_hidden + lax.psum_scatter(
-        (
-            matmul_nt(grad_query, query_weight)
-            + matmul_nt(grad_key, key_weight)
-            + matmul_nt(grad_value, value_weight)
-        ).astype(jnp.bfloat16),
-        "tensor",
-        scatter_dimension=0,
-        tiled=True,
-    ).astype(jnp.float32)
-    summed_attn_gain, summed_mlp_gain = (
-        lax.psum_scatter(part_attn_gain, ("dp", "tensor"), scatter_dimension=0, tiled=True),
-        lax.psum_scatter(part_mlp_gain, ("dp", "tensor"), scatter_dimension=0, tiled=True),
-    )
-    (
-        summed_query,
-        summed_key,
-        summed_value,
-        summed_out,
-        summed_query_gain,
-        summed_key_gain,
-        summed_gate,
-        summed_up,
-        summed_down,
-    ) = (
-        lax.psum_scatter(term_query, "dp", scatter_dimension=0, tiled=True),
-        lax.psum_scatter(term_key, "dp", scatter_dimension=0, tiled=True),
-        lax.psum_scatter(term_value, "dp", scatter_dimension=0, tiled=True),
-        lax.psum_scatter(term_out, "dp", scatter_dimension=1, tiled=True),
-        lax.psum_scatter(term_query_gain, "dp", scatter_dimension=1, tiled=True),
-        lax.psum_scatter(term_key_gain, "dp", scatter_dimension=1, tiled=True),
-        lax.psum_scatter(term_gate, "dp", scatter_dimension=0, tiled=True),
-        lax.psum_scatter(term_up, "dp", scatter_dimension=0, tiled=True),
-        lax.psum_scatter(term_down, "dp", scatter_dimension=1, tiled=True),
-    )
+    token_parts = by_owner(gathered, dp_size)
+    width = grad_query.shape[1]
+    grad_three = jnp.concatenate([grad_query, grad_key, grad_value], axis=1)
+    summed_three = reduce_product(
+        lambda part: matmul_tn(part, grad_three), *token_parts, 0, dp_size
+    )
+    summed_query, summed_key, summed_value = (
+        summed_three[:, :width],
+        summed_three[:, width : 2 * width],
+        summed_three[:, 2 * width :],
+    )
+    input_grad = grad_hidden + scatter_low(
+        matmul_nt(grad_query, query_weight)
+        + matmul_nt(grad_key, key_weight)
+        + matmul_nt(grad_value, value_weight)
+    )
+    place = lax.axis_index("dp")
+    summed_gains = add_all(
+        add_all(jnp.stack([part_attn_gain, part_mlp_gain]), "tensor", tensor_size), "dp", dp_size
+    )
+    summed_gains = own_part(
+        summed_gains,
+        1,
+        place * tensor_size + lax.axis_index("tensor"),
+        dp_size * tensor_size,
+    )
+    summed_attn_gain, summed_mlp_gain = summed_gains[0], summed_gains[1]
+    head_gains = own_part(
+        add_all(jnp.stack([term_query_gain, term_key_gain]), "dp", dp_size), 2, place, dp_size
+    )
+    summed_query_gain, summed_key_gain = head_gains[0], head_gains[1]
     return (
         output,
         input_grad,
@@ -305,7 +376,7 @@
         P(("dp", "tensor"), None),
     )
     return jax.shard_map(
-        on_device,
+        functools.partial(on_device, mesh.shape["dp"], mesh.shape["tensor"]),
         mesh=mesh,
         in_specs=placed,
         out_specs=(

time: 1270 us -> 643 us (0.51)
  waiting for transfers between devices: 964 us -> 315 us
  blocking collectives: 61.7 us -> 22.2 us
  starting transfers between devices: 2 us -> 31.8 us
  local copies, waits for them, and re-layouts: 35 us -> 60.5 us
  other arithmetic: 23.3 us -> 45.1 us
  matrix products: 163 us -> 145 us
    reduce_scatter x11 -> x4, waiting for transfers between devices: 776 us -> 95 us  [scatter_low(): lax.psum_scatter(values.astype(jnp.bfloat16), 'tensor', scatter_dimension...]
    ppermute x0 -> x33, waiting for transfers between devices: none -> 85.9 us  [the longest x25 57.4 us: exchange(): return lax.ppermute(values, 'dp', swap_pairs(size, step))]
    all_gather x1, waiting for transfers between devices: 46.1 us -> 0.01 us  [on_device(): grad_branch_rows = lax.all_gather(grad_branch, 'tensor', axis=0, tiled=True)]
    unnamed x1 -> x0, blocking collectives: 41.2 us -> none
    ppermute x0 -> x33, starting transfers between devices: none -> 30.4 us  [the longest x25 22.2 us: exchange(): return lax.ppermute(values, 'dp', swap_pairs(size, step))]
    add x1 -> x24, other arithmetic: 2.12 us -> 18.7 us  [the longest x15 15.3 us: halve(): lax.slice_in_dim(values, cut, 2 * cut, axis=axis)]
    dot_general x7 -> x10, matrix products: 57.2 us -> 44.6 us  [matmul_tn(): lax.dot_general(left, right, (((0,), (0,)), ((), ())), preferred_element_...]
    unnamed x97 -> x186, local copies, waits for them, and re-layouts: 19.3 us -> 30.4 us
  transfers between devices with their start and end apart: 17 -> 41, of which waited for: 14 -> 20; matrix products, arithmetic and copies ran while one was open for 7% -> 17% of each run, Pallas kernels for 0% -> 0%
where the time goes in v1:
time: 643 us; the launch traced here: 635 us
  waiting for transfers between devices  315 us (49%)
  matrix products  145 us (23%)
  local copies, waits for them, and re-layouts  60.5 us (9%)
  other arithmetic  45.1 us (7%)
  starting transfers between devices  31.8 us (5%)
  blocking collectives  22.2 us (3%)
  between operations  16 us (2%)
    reduce_scatter x4, waiting for transfers between devices, scatter_low(): lax.psum_scatter(values.astype(jnp.bfloat16), 'tensor', scatter_dimension...  95 us
    ppermute x25, waiting for transfers between devices, exchange(): return lax.ppermute(values, 'dp', swap_pairs(size, step))  57.4 us
    all_gather x1, waiting for transfers between devices, on_device(): gathered = lax.all_gather(tokens, 'tensor', axis=0, tiled=True)  48.7 us
    all_gather x1, waiting for transfers between devices, on_device(): lax.all_gather(hidden.astype(jnp.bfloat16), 'tensor', axis=0, tiled=True)  44.8 us
    dot_general x10, matrix products, matmul_tn(): lax.dot_general(left, right, (((0,), (0,)), ((), ())), preferred_element_...  44.6 us
    dot_general x7, matrix products, matmul(): return jnp.dot(left, right, preferred_element_type=jnp.float32)  40.3 us
    all_gather x1, waiting for transfers between devices, on_device(): grad_mlp_rows = lax.all_gather(grad_mlp, 'tensor', axis=0, tiled=True)  39.5 us
    dot_general x7, matrix products, matmul_nt(): lax.dot_general(left, right, (((1,), (1,)), ((), ())), preferred_element_...  39.4 us
  transfers between devices with their start and end apart: 41, of which 20 were waited for; matrix products, arithmetic and copies ran while one was open for 17% of the time, Pallas kernels for 0%

profile of v1, /device:TPU:0, one launch (start us, length us, event | category | flops | bytes accessed | tf_op | source)
XLA Modules:
  0.0 635.4 jit_solution(1312048170816330287)
XLA Ops:
  9.2 48.7 %all-gather.5.cloned.1.call-done = bf16[512,2048]{1,0:T(8,128)(2,1)} async-done(((bf16[128,2048]{1,0:T(8,128)(2,1)}), bf16[512,2048]{1,0:T(8,128)(2,1)}) %all-gather.5.cloned.1.call-update) | async-done | bytes 2097168 | tf_op jit(solution)/shard_map/all_gather | solution.py:234
  58.0 3.7 multiply_reduce_fusion.3
  61.7 2.3 multiply_reduce_fusion.4
  64.0 9.8 %all-reduce.1 = (f32[512]{0:T(512)S(1)}, f32[512]{0:T(512)S(1)}) all-reduce(f32[512]{0:T(512)S(1)} %get-tuple-element.167, f32[512]{0:T(512)S(1)} %get-tuple-element.169), channel_id=1, replica_groups=mesh['dp'=8,'tensor'=4] {'tensor'}, use_global_device_ids=true, to_apply=%region_1.2 | all-reduce | flops 1024 | bytes 8192 | tf_op jit(solution)/shard_map/psum | solution.py:240
  78.4 4.3 convolution_convert_fusion.8
  88.8 4.2 convolution_convert_fusion.5
  93.1 41.9 %reduce-scatter.5.cloned.1.call-done = bf16[128,2048]{1,0:T(8,128)(2,1)} async-done(((bf16[512,2048]{1,0:T(8,128)(2,1)}), bf16[128,2048]{1,0:T(8,128)(2,1)}) %reduce-scatter.5.cloned.1.call-update) | async-done | bytes 524304 | tf_op jit(solution)/shard_map/reduce_scatter | solution.py:208
  138.6 44.8 %all-gather.7.cloned.1.call-done = bf16[512,2048]{1,0:T(8,128)(2,1)} async-done(((bf16[128,2048]{1,0:T(8,128)(2,1)}), bf16[512,2048]{1,0:T(8,128)(2,1)}) %all-gather.7.cloned.1.call-update) | async-done | bytes 2097168 | tf_op jit(solution)/shard_map/all_gather | solution.py:253
  183.4 8.5 %fusion.106 = f32[512,2048]{1,0:T(8,128)S(1)} fusion(bf16[512,2048]{1,0:T(8,128)(2,1)} %all-gather.7.cloned.1.call-done, bf16[2048,2048]{1,0:T(8,128)(2,1)} %param.21), kind=kOutput, calls=%fused_computation.281 | convolution fusion | flops 4294967296 | bytes 14680064 | tf_op jit(solution)/shard_map/dot_general | solution.py:17
  191.9 11.7 %multiply_convert_fusion.2 = (bf16[512,2048]{1,0:T(8,128)(2,1)S(1)}, f32[512,2048]{1,0:T(8,128)}) fusion(f32[512,2048]{1,0:T(8,128)S(1)} %fusion.106, bf16[512,2048]{1,0:T(8,128)(2,1)S(1)} %copy-done.40, bf16[2048,2048]{1,0:T(8,128)(2,1)} %param.22), kind=kOutput, calls=%fused_computation.9 | convolution fusion | flops 4301258752 | bytes 20971520 | tf_op jit(solution)/shard_map/dot_general | solution.py:17
  204.9 5.7 convolution_convert_fusion.4
  210.7 42.5 %reduce-scatter.7.cloned.1.call-done = bf16[128,2048]{1,0:T(8,128)(2,1)} async-done(((bf16[512,2048]{1,0:T(8,128)(2,1)}), bf16[128,2048]{1,0:T(8,128)(2,1)}) %reduce-scatter.7.cloned.1.call-update) | async-done | bytes 524304 | tf_op jit(solution)/shard_map/reduce_scatter | solution.py:208
  262.6 39.5 %all-gather.9.cloned.1.call-done = bf16[512,2048]{1,0:T(8,128)(2,1)} async-done(((bf16[128,2048]{1,0:T(8,128)(2,1)}), bf16[512,2048]{1,0:T(8,128)(2,1)}) %all-gather.9.cloned.1.call-update) | async-done | bytes 2097168 | tf_op jit(solution)/shard_map/all_gather | solution.py:264
  302.1 11.9 %multiply_convert_fusion = (bf16[512,2048]{1,0:T(8,128)(2,1)S(1)}, bf16[512,2048]{1,0:T(8,128)(2,1)S(1)}) fusion(f32[512,2048]{1,0:T(8,128)} %copy-done.75, f32[512,2048]{1,0:T(8,128)} %get-tuple-element.174, bf16[512,2048]{1,0:T(8,128)(2,1)} %all-gather.9.cloned.1.call-done, bf16[2048,2048]{1,0:T(8,128)(2,1)} %param.23), kind=kOutput, calls=%fused_computation.7 | convolution fusion | flops 4308598784 | bytes 23068672 | tf_op jit(solution)/shard_map/dot_general | solution.py:21
  314.0 8.5 %fusion.107 = f32[512,2048]{1,0:T(8,128)S(1)} fusion(bf16[512,2048]{1,0:T(8,128)(2,1)S(1)} %get-tuple-element.64, bf16[2048,2048]{1,0:T(8,128)(2,1)} %param.21), kind=kOutput, calls=%fused_computation.282 | convolution fusion | flops 4294967296 | bytes 14680064 | tf_op jit(solution)/shard_map/dot_general | solution.py:21
  322.5 9.2 %add_convert_fusion.1 = bf16[512,2048]{1,0:T(8,128)(2,1)} fusion(f32[512,2048]{1,0:T(8,128)S(1)} %fusion.107, bf16[512,2048]{1,0:T(8,128)(2,1)S(1)} %get-tuple-element.63, bf16[2048,2048]{1,0:T(8,128)(2,1)} %param.22), kind=kOutput, calls=%fused_computation.6 | convolution fusion | flops 4297064448 | bytes 16777216 | tf_op jit(solution)/shard_map/dot_general | solution.py:21
  342.8 5.8 convolution_convert_fusion.2
  351.0 5.8 convolution_convert_fusion.1
  359.4 4.4 convolution_convert_fusion
  363.8 10.5 %reduce-scatter.9.cloned.1.call-done = bf16[128,2048]{1,0:T(8,128)(2,1)} async-done(((bf16[512,2048]{1,0:T(8,128)(2,1)}), bf16[128,2048]{1,0:T(8,128)(2,1)}) %reduce-scatter.9.cloned.1.call-update) | async-done | bytes 524304 | tf_op jit(solution)/shard_map/reduce_scatter | solution.py:208
  378.8 5.6 fusion.98
  390.4 5.0 fusion.97
  399.8 5.4 fusion.96
  405.2 27.7 %collective-permute-done.16 = f32[2,2048]{1,0:T(2,128)} collective-permute-done((f32[2,2048]{1,0:T(2,128)S(1)}, f32[2,2048]{1,0:T(2,128)}, u32[]{:S(2)}, u32[]{:S(2)}) %collective-permute-start.16) | collective-permute-done | bytes 16416 | tf_op jit(solution)/shard_map/ppermute | solution.py:197
  441.0 2.5 slice_add_fusion.5
  446.3 2.2 slice_add_fusion.3
  450.2 13.5 %collective-permute-done.29 = bf16[2048,256]{0,1:T(8,128)(2,1)S(1)} collective-permute-done((bf16[2048,256]{0,1:T(8,128)(2,1)}, bf16[2048,256]{0,1:T(8,128)(2,1)S(1)}, u32[]{:S(2)}, u32[]{:S(2)}) %collective-permute-start.29) | collective-permute-done | bytes 1048608 | tf_op jit(solution)/shard_map/ppermute | solution.py:168
  468.7 6.2 collective-permute-done.22
  477.1 9.0 %collective-permute-done.27 = bf16[128,2048]{1,0:T(8,128)(2,1)S(1)} collective-permute-done((bf16[128,2048]{1,0:T(8,128)(2,1)S(1)}, bf16[128,2048]{1,0:T(8,128)(2,1)S(1)}, u32[]{:S(2)}, u32[]{:S(2)}) %collective-permute-start.27) | collective-permute-done | bytes 524320 | tf_op jit(solution)/shard_map/ppermute | solution.py:168
  490.9 2.5 collective-permute-done.32
  496.2 4.5 convolution_convert_fusion.7
  504.8 2.9 fusion.66
  507.7 6.0 fusion.15
  513.7 6.0 fusion.12
  519.7 3.3 fusion.23
  524.8 3.0 reshape_reshape.7
  527.8 3.0 copy.48
  530.9 3.0 reshape_reshape.6
  539.6 12.4 %all-reduce = (f32[512]{0:T(512)S(1)}, f32[512]{0:T(512)S(1)}) all-reduce(f32[512]{0:T(512)S(1)} %get-tuple-element.42, f32[512]{0:T(512)S(1)} %get-tuple-element.44), channel_id=1, replica_groups=mesh['dp'=8,'tensor'=4] {'tensor'}, use_global_device_ids=true, to_apply=%region_15.16 | all-reduce | flops 1024 | bytes 8192 | tf_op jit(solution)/shard_map/psum | solution.py:299
  556.9 3.5 convolution_convert_fusion.3
  565.3 2.7 add_convert_fusion
  568.9 3.1 pad_maximum_fusion.1
  573.5 3.4 fusion.105
  581.1 3.2 copy.56
  589.3 3.8 fusion.104
  597.2 16.6 %collective-permute-done.10 = bf16[512,128]{1,0:T(8,128)(2,1)S(1)} collective-permute-done((bf16[512,128]{1,0:T(8,128)(2,1)S(1)}, bf16[512,128]{1,0:T(8,128)(2,1)S(1)}, u32[]{:S(2)}, u32[]{:S(2)}) %collective-permute-start.10) | collective-permute-done | bytes 131104 | tf_op jit(solution)/shard_map/ppermute | solution.py:168
  618.0 2.5 convert_add_fusion.5
  620.5 4.2 collective-permute-done.4
  (356 shorter events, 128.7 us)
Async XLA Ops:
  7.2 54.5 %copy-start = (bf16[2048,512]{1,0:T(8,128)(2,1)S(1)}, bf16[2048,512]{1,0:T(8,128)(2,1)}, u32[]{:S(2)}) copy-start(bf16[2048,512]{1,0:T(8,128)(2,1)} %param.14) | copy-start | bytes 6291460
  7.2 50.8 %all-gather.5.cloned.1.call-start = ((), (), s32[]{:S(2)}) async-start(), calls=%async_computation.4 | async-start | bytes 2621440 | tf_op jit(solution)/shard_map/all_gather | solution.py:234
  7.9 127.1 %reduce-scatter.5.cloned.1.call-start = ((), (), s32[]{:S(2)}) async-start(), calls=%async_computation.5 | async-start | bytes 2621440 | tf_op jit(solution)/shard_map/reduce_scatter | solution.py:208
  8.0 78.1 %copy-start.60 = (pred[256,256]{0,1:T(8,128)(4,1)}, pred[256,256]{0,1:T(8,128)(4,1)S(1)}, u32[]{:S(2)}) copy-start(pred[256,256]{0,1:T(8,128)(4,1)S(1)} %iota_compare_fusion) | copy-start | bytes 196612
  93.0 43.3 %copy-start.25 = (bf16[128,2048]{1,0:T(8,128)(2,1)S(1)}, bf16[128,2048]{1,0:T(8,128)(2,1)}, u32[]{:S(2)}) copy-start(bf16[128,2048]{1,0:T(8,128)(2,1)} %param.13) | copy-start | bytes 1572868
  93.0 43.3 %copy-start.62 = (f32[2048]{0:T(1024)S(1)}, f32[2048]{0:T(1024)}, u32[]{:S(2)}) copy-start(f32[2048]{0:T(1024)} %param.20) | copy-start | bytes 24580
  93.0 90.4 %all-gather.7.cloned.1.call-start = ((), (), s32[]{:S(2)}) async-start(), calls=%async_computation.6 | async-start | bytes 2621440 | tf_op jit(solution)/shard_map/all_gather | solution.py:253
  138.4 114.9 %reduce-scatter.7.cloned.1.call-start = ((), (), s32[]{:S(2)}) async-start(), calls=%async_computation.7 | async-start | bytes 2621440 | tf_op jit(solution)/shard_map/reduce_scatter | solution.py:208
  183.4 21.5 %slice-start = ((s8[8388608]{0:T(1024)(128)(4,1)}), s8[4194304]{0:T(1024)(128)(4,1)S(1)}, s32[]{:S(2)}) async-start(s8[8388608]{0:T(1024)(128)(4,1)} %bitcast.156), calls=%async_computation.12 | async-start | bytes 8388608
  210.6 43.9 %copy-start.1 = (f32[128,2048]{1,0:T(8,128)S(1)}, f32[128,2048]{1,0:T(8,128)}, u32[]{:S(2)}) copy-start(f32[128,2048]{1,0:T(8,128)} %param.25) | copy-start | bytes 3145732
  210.6 43.9 %copy-start.63 = (f32[2048]{0:T(1024)S(1)}, f32[2048]{0:T(1024)}, u32[]{:S(2)}) copy-start(f32[2048]{0:T(1024)} %param.24) | copy-start | bytes 24580
  210.7 91.4 %all-gather.9.cloned.1.call-start = ((), (), s32[]{:S(2)}) async-start(), calls=%async_computation.8 | async-start | bytes 2621440 | tf_op jit(solution)/shard_map/all_gather | solution.py:264
  257.1 117.2 %reduce-scatter.9.cloned.1.call-start = ((), (), s32[]{:S(2)}) async-start(), calls=%async_computation.9 | async-start | bytes 2621440 | tf_op jit(solution)/shard_map/reduce_scatter | solution.py:208
  331.7 164.5 %all-gather.11.cloned.1.call-start = ((), (), s32[]{:S(2)}) async-start(), calls=%async_computation.10 | async-start | bytes 2621440 | tf_op jit(solution)/shard_map/all_gather | solution.py:283
  348.7 30.1 %collective-permute-start.18 = (bf16[1024,2048]{1,0:T(8,128)(2,1)}, bf16[1024,2048]{1,0:T(8,128)(2,1)}, u32[]{:S(2)}, u32[]{:S(2)}) collective-permute-start(bf16[1024,2048]{1,0:T(8,128)(2,1)} %convolution_convert_fusion.2), channel_id=1, source_target_pairs={{0,4},{4,0},{8,12},{12,8},{16,20},{20,16},{24,28},{28,24},{1,5},{5... | collective-permute-start | bytes 12582920 | tf_op jit(solution)/shard_map/ppermute | solution.py:168
  356.8 33.6 %collective-permute-start.23 = (bf16[1024,2048]{1,0:T(8,128)(2,1)}, bf16[1024,2048]{1,0:T(8,128)(2,1)}, u32[]{:S(2)}, u32[]{:S(2)}) collective-permute-start(bf16[1024,2048]{1,0:T(8,128)(2,1)} %convolution_convert_fusion.1), channel_id=1, source_target_pairs={{0,4},{4,0},{8,12},{12,8},{16,20},{20,16},{24,28},{28,24},{1,5},{5... | collective-permute-start | bytes 12582920 | tf_op jit(solution)/shard_map/ppermute | solution.py:168
  363.8 34.6 %collective-permute-start.28 = (bf16[2048,1024]{0,1:T(8,128)(2,1)}, bf16[2048,1024]{0,1:T(8,128)(2,1)}, u32[]{:S(2)}, u32[]{:S(2)}) collective-permute-start(bf16[2048,1024]{0,1:T(8,128)(2,1)} %convolution_convert_fusion), channel_id=1, source_target_pairs={{0,4},{4,0},{8,12},{12,8},{16,20},{20,16},{24,28},{28,24},{1,5},{5... | collective-permute-start | bytes 12582920 | tf_op jit(solution)/shard_map/ppermute | solution.py:168
  377.8 240.1 %reduce-scatter.11.cloned.1.call-start = ((), (), s32[]{:S(2)}) async-start(), calls=%async_computation.11 | async-start | bytes 2621440 | tf_op jit(solution)/shard_map/reduce_scatter | solution.py:208
  378.1 10.8 %collective-permute-start.13 = (f32[2,2048]{1,0:T(2,128)S(1)}, f32[2,2048]{1,0:T(2,128)S(1)}, u32[]{:S(2)}, u32[]{:S(2)}) collective-permute-start(f32[2,2048]{1,0:T(2,128)S(1)} %pad_maximum_fusion.14), channel_id=1, source_target_pairs={{0,1},{1,0},{2,3},{3,2},{4,5},{5,4},{6,7},{7,6},{8,9},{9,8},{10,11... | collective-permute-start | bytes 49160 | tf_op jit(solution)/shard_map/ppermute | solution.py:197
  385.9 53.6 %collective-permute-start.19 = (bf16[256,2048]{1,0:T(8,128)(2,1)}, bf16[256,2048]{1,0:T(8,128)(2,1)}, u32[]{:S(2)}, u32[]{:S(2)}) collective-permute-start(bf16[256,2048]{1,0:T(8,128)(2,1)} %get-tuple-element.71), channel_id=1, source_target_pairs={{0,8},{4,12},{8,0},{12,4},{16,24},{20,28},{24,16},{28,20},{1,9},{5... | collective-permute-start | bytes 3145736 | tf_op jit(solution)/shard_map/ppermute | solution.py:168
  387.4 53.6 %collective-permute-start.21 = (bf16[256,2048]{1,0:T(8,128)(2,1)}, bf16[256,2048]{1,0:T(8,128)(2,1)}, u32[]{:S(2)}, u32[]{:S(2)}) collective-permute-start(bf16[256,2048]{1,0:T(8,128)(2,1)} %get-tuple-element.72), channel_id=1, source_target_pairs={{0,16},{4,20},{8,24},{12,28},{16,0},{20,4},{24,8},{28,12},{1,17},{... | collective-permute-start | bytes 3145736 | tf_op jit(solution)/shard_map/ppermute | solution.py:168
  388.9 6.6 %collective-permute-start.14 = (f32[2,2048]{1,0:T(2,128)S(1)}, f32[2,2048]{1,0:T(2,128)S(1)}, u32[]{:S(2)}, u32[]{:S(2)}) collective-permute-start(f32[2,2048]{1,0:T(2,128)S(1)} %fusion.95), channel_id=1, source_target_pairs={{0,2},{1,3},{2,0},{3,1},{4,6},{5,7},{6,4},{7,5},{8,10},{9,11},{10,... | collective-permute-start | bytes 49160 | tf_op jit(solution)/shard_map/ppermute | solution.py:197
  395.5 2.1 collective-permute-start.15
  397.0 48.7 %collective-permute-start.24 = (bf16[256,2048]{1,0:T(8,128)(2,1)}, bf16[256,2048]{1,0:T(8,128)(2,1)}, u32[]{:S(2)}, u32[]{:S(2)}) collective-permute-start(bf16[256,2048]{1,0:T(8,128)(2,1)} %get-tuple-element.69), channel_id=1, source_target_pairs={{0,8},{4,12},{8,0},{12,4},{16,24},{20,28},{24,16},{28,20},{1,9},{5... | collective-permute-start | bytes 3145736 | tf_op jit(solution)/shard_map/ppermute | solution.py:168
  397.6 48.7 %collective-permute-start.26 = (bf16[256,2048]{1,0:T(8,128)(2,1)}, bf16[256,2048]{1,0:T(8,128)(2,1)}, u32[]{:S(2)}, u32[]{:S(2)}) collective-permute-start(bf16[256,2048]{1,0:T(8,128)(2,1)} %get-tuple-element.70), channel_id=1, source_target_pairs={{0,16},{4,20},{8,24},{12,28},{16,0},{20,4},{24,8},{28,12},{1,17},{... | collective-permute-start | bytes 3145736 | tf_op jit(solution)/shard_map/ppermute | solution.py:168
  398.4 34.5 %collective-permute-start.16 = (f32[2,2048]{1,0:T(2,128)S(1)}, f32[2,2048]{1,0:T(2,128)}, u32[]{:S(2)}, u32[]{:S(2)}) collective-permute-start(f32[2,2048]{1,0:T(2,128)S(1)} %add.456), channel_id=1, source_target_pairs={{0,8},{4,12},{8,0},{12,4},{16,24},{20,28},{24,16},{28,20},{1,9},{5... | collective-permute-start | bytes 49160 | tf_op jit(solution)/shard_map/ppermute | solution.py:197
  433.6 3.8 collective-permute-start.17
  437.5 26.2 %collective-permute-start.29 = (bf16[2048,256]{0,1:T(8,128)(2,1)}, bf16[2048,256]{0,1:T(8,128)(2,1)S(1)}, u32[]{:S(2)}, u32[]{:S(2)}) collective-permute-start(bf16[2048,256]{0,1:T(8,128)(2,1)} %get-tuple-element.67), channel_id=1, source_target_pairs={{0,8},{4,12},{8,0},{12,4},{16,24},{20,28},{24,16},{28,20},{1,9},{5... | collective-permute-start | bytes 3145736 | tf_op jit(solution)/shard_map/ppermute | solution.py:168
  439.5 26.4 %collective-permute-start.31 = (bf16[2048,256]{0,1:T(8,128)(2,1)}, bf16[2048,256]{0,1:T(8,128)(2,1)}, u32[]{:S(2)}, u32[]{:S(2)}) collective-permute-start(bf16[2048,256]{0,1:T(8,128)(2,1)} %get-tuple-element.68), channel_id=1, source_target_pairs={{0,16},{4,20},{8,24},{12,28},{16,0},{20,4},{24,8},{28,12},{1,17},{... | collective-permute-start | bytes 3145736 | tf_op jit(solution)/shard_map/ppermute | solution.py:168
  444.3 30.6 %collective-permute-start.22 = (bf16[128,2048]{1,0:T(8,128)(2,1)}, bf16[128,2048]{1,0:T(8,128)(2,1)S(1)}, u32[]{:S(2)}, u32[]{:S(2)}) collective-permute-start(bf16[128,2048]{1,0:T(8,128)(2,1)} %slice.390), channel_id=1, source_target_pairs={{0,8},{4,12},{8,0},{12,4},{16,24},{20,28},{24,16},{28,20},{1,9},{5... | collective-permute-start | bytes 1572872 | tf_op jit(solution)/shard_map/ppermute | solution.py:168
  445.7 31.3 %collective-permute-start.20 = (bf16[128,2048]{1,0:T(8,128)(2,1)}, bf16[128,2048]{1,0:T(8,128)(2,1)S(1)}, u32[]{:S(2)}, u32[]{:S(2)}) collective-permute-start(bf16[128,2048]{1,0:T(8,128)(2,1)} %slice.391), channel_id=1, source_target_pairs={{0,16},{4,20},{8,24},{12,28},{16,0},{20,4},{24,8},{28,12},{1,17},{... | collective-permute-start | bytes 1572872 | tf_op jit(solution)/shard_map/ppermute | solution.py:168
  448.6 37.6 %collective-permute-start.27 = (bf16[128,2048]{1,0:T(8,128)(2,1)S(1)}, bf16[128,2048]{1,0:T(8,128)(2,1)S(1)}, u32[]{:S(2)}, u32[]{:S(2)}) collective-permute-start(bf16[128,2048]{1,0:T(8,128)(2,1)S(1)} %slice.388), channel_id=1, source_target_pairs={{0,8},{4,12},{8,0},{12,4},{16,24},{20,28},{24,16},{28,20},{1,9},{5... | collective-permute-start | bytes 1572872 | tf_op jit(solution)/shard_map/ppermute | solution.py:168
  463.7 24.5 %collective-permute-start.25 = (bf16[128,2048]{1,0:T(8,128)(2,1)S(1)}, bf16[128,2048]{1,0:T(8,128)(2,1)S(1)}, u32[]{:S(2)}, u32[]{:S(2)}) collective-permute-start(bf16[128,2048]{1,0:T(8,128)(2,1)S(1)} %slice.389), channel_id=1, source_target_pairs={{0,16},{4,20},{8,24},{12,28},{16,0},{20,4},{24,8},{28,12},{1,17},{... | collective-permute-start | bytes 1572872 | tf_op jit(solution)/shard_map/ppermute | solution.py:168
  467.8 25.5 %collective-permute-start.32 = (bf16[2048,128]{0,1:T(8,128)(2,1)S(1)}, bf16[2048,128]{0,1:T(8,128)(2,1)S(1)}, u32[]{:S(2)}, u32[]{:S(2)}) collective-permute-start(bf16[2048,128]{0,1:T(8,128)(2,1)S(1)} %slice.386), channel_id=1, source_target_pairs={{0,8},{4,12},{8,0},{12,4},{16,24},{20,28},{24,16},{28,20},{1,9},{5... | collective-permute-start | bytes 1572872 | tf_op jit(solution)/shard_map/ppermute | solution.py:168
  474.9 20.1 %collective-permute-start.30 = (bf16[2048,128]{0,1:T(8,128)(2,1)S(1)}, bf16[2048,128]{0,1:T(8,128)(2,1)S(1)}, u32[]{:S(2)}, u32[]{:S(2)}) collective-permute-start(bf16[2048,128]{0,1:T(8,128)(2,1)S(1)} %slice.387), channel_id=1, source_target_pairs={{0,16},{4,20},{8,24},{12,28},{16,0},{20,4},{24,8},{28,12},{1,17},{... | collective-permute-start | bytes 1572872 | tf_op jit(solution)/shard_map/ppermute | solution.py:168
  560.4 28.9 %collective-permute-start = (bf16[1024,1536]{1,0:T(8,128)(2,1)}, bf16[1024,1536]{1,0:T(8,128)(2,1)}, u32[]{:S(2)}, u32[]{:S(2)}) collective-permute-start(bf16[1024,1536]{1,0:T(8,128)(2,1)} %convolution_convert_fusion.3), channel_id=1, source_target_pairs={{0,4},{4,0},{8,12},{12,8},{16,20},{20,16},{24,28},{28,24},{1,5},{5... | collective-permute-start | bytes 9437192 | tf_op jit(solution)/shard_map/ppermute | solution.py:168
  560.4 7.6 %collective-permute-start.5 = (f32[2,4,128]{2,1,0:T(4,128)S(1)}, f32[2,4,128]{2,1,0:T(4,128)S(1)}, u32[]{:S(2)}, u32[]{:S(2)}) collective-permute-start(f32[2,4,128]{2,1,0:T(4,128)S(1)} %pad_maximum_fusion.15), channel_id=1, source_target_pairs={{0,4},{4,0},{8,12},{12,8},{16,20},{20,16},{24,28},{28,24},{1,5},{5... | collective-permute-start | bytes 12296 | tf_op jit(solution)/shard_map/ppermute | solution.py:197
  563.7 9.8 %collective-permute-start.8 = (bf16[512,1024]{1,0:T(8,128)(2,1)}, bf16[512,1024]{1,0:T(8,128)(2,1)}, u32[]{:S(2)}, u32[]{:S(2)}) collective-permute-start(bf16[512,1024]{1,0:T(8,128)(2,1)} %convolution_convert_fusion.6), channel_id=1, source_target_pairs={{0,4},{4,0},{8,12},{12,8},{16,20},{20,16},{24,28},{28,24},{1,5},{5... | collective-permute-start | bytes 3145736 | tf_op jit(solution)/shard_map/ppermute | solution.py:168
  568.1 4.0 collective-permute-start.6
  572.0 12.3 %collective-permute-start.7 = (f32[2,4,128]{2,1,0:T(4,128)S(1)}, f32[2,4,128]{2,1,0:T(4,128)S(1)}, u32[]{:S(2)}, u32[]{:S(2)}) collective-permute-start(f32[2,4,128]{2,1,0:T(4,128)S(1)} %fusion.156), channel_id=1, source_target_pairs={{0,16},{4,20},{8,24},{12,28},{16,0},{20,4},{24,8},{28,12},{1,17},{... | collective-permute-start | bytes 12296 | tf_op jit(solution)/shard_map/ppermute | solution.py:197
  577.8 8.1 %collective-permute-start.9 = (bf16[512,256]{1,0:T(8,128)(2,1)}, bf16[512,256]{1,0:T(8,128)(2,1)S(1)}, u32[]{:S(2)}, u32[]{:S(2)}) collective-permute-start(bf16[512,256]{1,0:T(8,128)(2,1)} %get-tuple-element.152), channel_id=1, source_target_pairs={{0,8},{4,12},{8,0},{12,4},{16,24},{20,28},{24,16},{28,20},{1,9},{5... | collective-permute-start | bytes 786440 | tf_op jit(solution)/shard_map/ppermute | solution.py:168
  579.0 7.9 %collective-permute-start.11 = (bf16[512,256]{1,0:T(8,128)(2,1)}, bf16[512,256]{1,0:T(8,128)(2,1)}, u32[]{:S(2)}, u32[]{:S(2)}) collective-permute-start(bf16[512,256]{1,0:T(8,128)(2,1)} %get-tuple-element.153), channel_id=1, source_target_pairs={{0,16},{4,20},{8,24},{12,28},{16,0},{20,4},{24,8},{28,12},{1,17},{... | collective-permute-start | bytes 786440 | tf_op jit(solution)/shard_map/ppermute | solution.py:168
  588.4 8.8 %collective-permute-start.12 = (bf16[512,128]{1,0:T(8,128)(2,1)S(1)}, bf16[512,128]{1,0:T(8,128)(2,1)S(1)}, u32[]{:S(2)}, u32[]{:S(2)}) collective-permute-start(bf16[512,128]{1,0:T(8,128)(2,1)S(1)} %slice.394), channel_id=1, source_target_pairs={{0,8},{4,12},{8,0},{12,4},{16,24},{20,28},{24,16},{28,20},{1,9},{5... | collective-permute-start | bytes 393224 | tf_op jit(solution)/shard_map/ppermute | solution.py:168
  593.2 21.4 %collective-permute-start.3 = (bf16[256,1536]{1,0:T(8,128)(2,1)S(1)}, bf16[256,1536]{1,0:T(8,128)(2,1)S(1)}, u32[]{:S(2)}, u32[]{:S(2)}) collective-permute-start(bf16[256,1536]{1,0:T(8,128)(2,1)S(1)} %get-tuple-element.73), channel_id=1, source_target_pairs={{0,16},{4,20},{8,24},{12,28},{16,0},{20,4},{24,8},{28,12},{1,17},{... | collective-permute-start | bytes 2359304 | tf_op jit(solution)/shard_map/ppermute | solution.py:168
  593.9 20.7 %collective-permute-start.1 = (bf16[256,1536]{1,0:T(8,128)(2,1)S(1)}, bf16[256,1536]{1,0:T(8,128)(2,1)S(1)}, u32[]{:S(2)}, u32[]{:S(2)}) collective-permute-start(bf16[256,1536]{1,0:T(8,128)(2,1)S(1)} %get-tuple-element.74), channel_id=1, source_target_pairs={{0,8},{4,12},{8,0},{12,4},{16,24},{20,28},{24,16},{28,20},{1,9},{5... | collective-permute-start | bytes 2359304 | tf_op jit(solution)/shard_map/ppermute | solution.py:168
  595.7 18.0 %collective-permute-start.10 = (bf16[512,128]{1,0:T(8,128)(2,1)S(1)}, bf16[512,128]{1,0:T(8,128)(2,1)S(1)}, u32[]{:S(2)}, u32[]{:S(2)}) collective-permute-start(bf16[512,128]{1,0:T(8,128)(2,1)S(1)} %slice.395), channel_id=1, source_target_pairs={{0,16},{4,20},{8,24},{12,28},{16,0},{20,4},{24,8},{28,12},{1,17},{... | collective-permute-start | bytes 393224 | tf_op jit(solution)/shard_map/ppermute | solution.py:168
  616.0 8.7 %collective-permute-start.4 = (bf16[128,1536]{1,0:T(8,128)(2,1)}, bf16[128,1536]{1,0:T(8,128)(2,1)}, u32[]{:S(2)}, u32[]{:S(2)}) collective-permute-start(bf16[128,1536]{1,0:T(8,128)(2,1)} %slice.392), channel_id=1, source_target_pairs={{0,8},{4,12},{8,0},{12,4},{16,24},{20,28},{24,16},{28,20},{1,9},{5... | collective-permute-start | bytes 1179656 | tf_op jit(solution)/shard_map/ppermute | solution.py:168
  617.3 8.5 %collective-permute-start.2 = (bf16[128,1536]{1,0:T(8,128)(2,1)S(1)}, bf16[128,1536]{1,0:T(8,128)(2,1)}, u32[]{:S(2)}, u32[]{:S(2)}) collective-permute-start(bf16[128,1536]{1,0:T(8,128)(2,1)S(1)} %slice.393), channel_id=1, source_target_pairs={{0,16},{4,20},{8,24},{12,28},{16,0},{20,4},{24,8},{28,12},{1,17},{... | collective-permute-start | bytes 1179656 | tf_op jit(solution)/shard_map/ppermute | solution.py:168
  (71 other events, 290.7 us)
Sparse Core Ops, SparseCore 0:
  9.6 48.3 all-gather.4
  93.1 41.8 reduce-scatter.4
  138.5 44.8 all-gather.6
  210.8 42.4 reduce-scatter.6
  257.2 44.8 all-gather.8
  331.8 42.4 reduce-scatter.8
  377.9 45.5 all-gather.10
  568.1 41.0 reduce-scatter.10

commit v2 on v1

v2 whole, which is shorter than its diff:
```python
import functools
import math

import jax
import jax.numpy as jnp
from jax import lax
from jax.experimental import pallas as pl
from jax.experimental.pallas import tpu as pltpu
from jax.sharding import PartitionSpec as P

L = 256


rms_eps = 1e-06
rope_base = 500000.0


def matmul(left, right):
    return jnp.dot(left, right, preferred_element_type=jnp.float32)


def matmul_nt(left, right):
    return lax.dot_general(
        left, right, (((1,), (1,)), ((), ())), preferred_element_type=jnp.float32
    )


def matmul_tn(left, right):
    return lax.dot_general(
        left, right, (((0,), (0,)), ((), ())), preferred_element_type=jnp.float32
    )


def rope_tables(row_total, half_dim):
    places = (jnp.arange(row_total, dtype=jnp.int32) % L).astype(jnp.float32)
    powers = jnp.arange(half_dim, dtype=jnp.int32).astype(jnp.float32) * (2.0 / (2 * half_dim))
    frequency = jnp.exp(-math.log(rope_base) * powers)
    angles = places[:, None] * frequency[None, :]
    return (jnp.cos(angles), jnp.sin(angles))


def rms_scale(values):
    return lax.rsqrt(jnp.mean(values * values, axis=-1, keepdims=True) + rms_eps)


def norm_back(values, scales, gain_row, upstream):
    weighted = upstream * gain_row
    inner_mean = jnp.mean(weighted * values, axis=-1, keepdims=True)
    return scales * (weighted - values * scales * scales * inner_mean)


def swap_halves(values):
    return pltpu.roll(values, values.shape[1] // 2, 1)


def causal_scores(query_rot, key_rot):
    scores = matmul_nt(query_rot, key_rot) * (1.0 / math.sqrt(query_rot.shape[1]))
    row = lax.broadcasted_iota(jnp.int32, scores.shape, 0)
    column = lax.broadcasted_iota(jnp.int32, scores.shape, 1)
    masked = jnp.where(row >= column, scores, -jnp.inf)
    expo_vals = jnp.exp(masked - jnp.max(masked, axis=-1, keepdims=True))
    return expo_vals / jnp.sum(expo_vals, axis=-1, keepdims=True)


def attend_kernel(
    query_ref,
    key_ref,
    value_ref,
    query_scale_ref,
    key_scale_ref,
    query_gain_ref,
    key_gain_ref,
    cosine_ref,
    sine_ref,
    attended_ref,
    query_rot_ref,
    key_rot_ref,
):
    def turned(values_ref, scale_ref, gain_ref):
        normed = values_ref[...] * scale_ref[...] * gain_ref[...]
        return (normed * cosine_ref[...] + swap_halves(normed) * sine_ref[...]).astype(jnp.bfloat16)

    query_rot = turned(query_ref, query_scale_ref, query_gain_ref)
    key_rot = turned(key_ref, key_scale_ref, key_gain_ref)
    probability = causal_scores(query_rot, key_rot).astype(jnp.bfloat16)
    attended_ref[...] = matmul(probability, value_ref[...]).astype(jnp.bfloat16)
    query_rot_ref[...] = query_rot
    key_rot_ref[...] = key_rot


def attend_back_kernel(
    upstream_ref,
    query_rot_ref,
    key_rot_ref,
    value_ref,
    query_ref,
    key_ref,
    query_scale_ref,
    key_scale_ref,
    query_gain_ref,
    key_gain_ref,
    cosine_ref,
    sine_ref,
    grad_query_ref,
    grad_key_ref,
    grad_value_ref,
    query_inner_ref,
    key_inner_ref,
    query_term_ref,
    key_term_ref,
):
    query_rot, key_rot, upstream = query_rot_ref[...], key_rot_ref[...], upstream_ref[...]
    prob_full = causal_scores(query_rot, key_rot)
    grad_value_ref[...] = matmul_tn(prob_full.astype(jnp.bfloat16), upstream).astype(jnp.bfloat16)
    grad_prob = matmul_nt(upstream, value_ref[...])
    row_dot = jnp.sum(prob_full * grad_prob, axis=-1, keepdims=True)
    factor = 1.0 / math.sqrt(query_rot.shape[1])
    grad_scores = (prob_full * (grad_prob - row_dot) * factor).astype(jnp.bfloat16)

    def back(grad_rot, values_ref, scale_ref, gain_ref, grad_ref, inner_ref, term_ref):
        grad_normed = grad_rot * cosine_ref[...] - swap_halves(grad_rot) * sine_ref[...]
        values = values_ref[...]
        weighted = grad_normed * gain_ref[...]
        grad_ref[...] = weighted
        term_ref[0] = jnp.sum(grad_normed * values * scale_ref[...], axis=0, keepdims=True)
        inner = jnp.sum(weighted * values, axis=-1, keepdims=True)

        @pl.when(pl.program_id(1) == 0)
        def _():
            inner_ref[...] = inner

        @pl.when(pl.program_id(1) > 0)
        def _():
            inner_ref[...] += inner

    back(
        matmul(grad_scores, key_rot),
        query_ref,
        query_scale_ref,
        query_gain_ref,
        grad_query_ref,
        query_inner_ref,
        query_term_ref,
    )
    back(
        matmul_tn(grad_scores, query_rot),
        key_ref,
        key_scale_ref,
        key_gain_ref,
        grad_key_ref,
        key_inner_ref,
        key_term_ref,
    )


def head_call(kernel, ins, out_shapes, head_dim):
    row_total, width = ins[0].shape
    grid = (row_total // L, width // head_dim)

    def spec(shape):
        if len(shape) == 3:
            return pl.BlockSpec((1, 1, head_dim), lambda s, h: (s, 0, h))
        if shape[0] == row_total and shape[1] == width:
            return pl.BlockSpec((L, head_dim), lambda s, h: (s, h))
        if shape[0] == row_total:
            return pl.BlockSpec((L, 1), lambda s, h: (s, 0))
        if shape[0] == 1:
            return pl.BlockSpec((1, head_dim), lambda s, h: (0, h))
        return pl.BlockSpec((L, head_dim), lambda s, h: (0, 0))

    return pl.pallas_call(
        kernel,
        grid=grid,
        out_shape=out_shapes,
        in_specs=[spec(member.shape) for member in ins],
        out_specs=[spec(member.shape) for member in out_shapes],
        cost_estimate=pl.CostEstimate(
            flops=8 * row_total * L * width, bytes_accessed=16 * row_total * width, transcendentals=0
        ),
    )(*ins)


def pick_kernel(part, order_ref, source_ref, target_ref):
    for place in range(target_ref.shape[1] // part):
        start = pl.multiple_of(order_ref[place] * part, part)
        target_ref[:, place * part : (place + 1) * part] = source_ref[:, pl.ds(start, part)]


def pick_blocks(columns, order, part):
    count = len(order)
    if part % 128:
        return jnp.concatenate(
            [lax.dynamic_slice_in_dim(columns, place * part, part, axis=1) for place in order],
            axis=1,
        )
    whole = pl.BlockSpec(memory_space=pltpu.VMEM)
    return pl.pallas_call(
        functools.partial(pick_kernel, part),
        in_specs=[pl.BlockSpec(memory_space=pltpu.SMEM), whole],
        out_specs=whole,
        out_shape=jax.ShapeDtypeStruct((columns.shape[0], count * part), columns.dtype),
        cost_estimate=pl.CostEstimate(
            flops=0, bytes_accessed=4 * columns.size, transcendentals=0
        ),
    )(jnp.stack(order), columns)


def swap_pairs(size, step):
    return [(place, place ^ step) for place in range(size)]


def owner_order(bits):
    if not bits:
        return [0]
    rest = owner_order(bits[1:])
    return [member | (1 << bits[0]) for member in rest] + rest


def half_plans(size):
    bits = list(range(1, size.bit_length() - 1))
    return bits, bits[1:] + bits[:1]


def by_owner(columns, size):
    me = lax.axis_index("dp")
    part = columns.shape[1] // size // 2
    order = [
        (me ^ (mask | flip)) * 2 + half
        for flip in (1, 0)
        for half, bits in enumerate(half_plans(size))
        for mask in owner_order(bits)
    ]
    picked = pick_blocks(columns, order, part)
    cut = columns.shape[1] // 2
    return picked[:, :cut], picked[:, cut:]


def exchange(values, size, step):
    return lax.ppermute(values, "dp", swap_pairs(size, step))


def halve(values, axis, size, bits):
    for bit in bits:
        cut = values.shape[axis] // 2
        sent = lax.slice_in_dim(values, 0, cut, axis=axis).astype(jnp.bfloat16)
        arrived = exchange(sent, size, 1 << bit)
        values = lax.slice_in_dim(values, cut, 2 * cut, axis=axis) + arrived.astype(jnp.float32)
    return values


def reduce_product(product, sent, kept, axis, size):
    arrived = exchange(product(sent).astype(jnp.bfloat16), size, 1)
    held = product(kept) + arrived.astype(jnp.float32)
    cut = held.shape[axis] // 2
    first, second = half_plans(size)
    return jnp.concatenate(
        [
            halve(lax.slice_in_dim(held, 0, cut, axis=axis), axis, size, first),
            halve(lax.slice_in_dim(held, cut, 2 * cut, axis=axis), axis, size, second),
        ],
        axis=axis,
    )


def add_all(values, name, size):
    step = 1
    while step < size:
        values = values + lax.ppermute(values, name, swap_pairs(size, step))
        step *= 2
    return values


def own_part(values, axis, place, count):
    part = values.shape[axis] // count
    return lax.dynamic_slice_in_dim(values, place * part, part, axis=axis)


STEPS = 8
LINE_COST = 3000


def line_kernel(size, steps, summed, spread, middle, in_count, out_count, *refs):
    me = lax.axis_index("tensor")
    first_ref = refs[0]
    ins = refs[1:in_count]
    outs = refs[in_count : in_count + out_count]
    scratch = list(refs[in_count + out_count :])
    all_rows = (first_ref if summed else outs[0]).shape[0]
    block = all_rows // size
    part = block // steps
    if summed:
        right_ref, left_ref, sum_sent, sum_come = scratch[:4]
        del scratch[:4]
    if spread:
        spread_sent, spread_come = scratch

    def rows(owner, chunk):
        return pl.ds(pl.multiple_of(owner * block + chunk * part, part), part)

    def mine(chunk):
        return pl.ds(pl.multiple_of(chunk * part, part), part)

    has_left, has_right = me > 0, me < size - 1
    right, left = jnp.minimum(me + 1, size - 1), jnp.maximum(me - 1, 0)

    barrier = pltpu.get_barrier_semaphore()

    @pl.when(has_left)
    def _():
        pl.semaphore_signal(
            barrier, inc=1, device_id={"tensor": left}, device_id_type=pl.DeviceIdType.MESH
        )

    @pl.when(has_right)
    def _():
        pl.semaphore_signal(
            barrier, inc=1, device_id={"tensor": right}, device_id_type=pl.DeviceIdType.MESH
        )

    pl.semaphore_wait(barrier, has_left.astype(jnp.int32) + has_right.astype(jnp.int32))

    def move(source, target, sent, come, device):
        return pltpu.make_async_remote_copy(
            src_ref=source,
            dst_ref=target,
            send_sem=sent,
            recv_sem=come,
            device_id={"tensor": device},
            device_id_type=pl.DeviceIdType.MESH,
        )

    def sum_copy(way, owner, chunk):
        held = (right_ref, left_ref)[way]
        place = held.at[rows(owner, chunk)]
        return move(
            place,
            place,
            sum_sent.at[way, owner, chunk],
            sum_come.at[way, owner, chunk],
            (right, left)[way],
        )

    def spread_copy(way, owner, chunk):
        place = outs[0].at[rows(owner, chunk)]
        return move(
            place,
            place,
            spread_sent.at[way, owner, chunk],
            spread_come.at[owner, chunk],
            (right, left)[way],
        )

    def sum_step(distance, chunk):
        for way in (0, 1):
            owner = me + distance if way == 0 else me - distance
            inside = owner < size if way == 0 else owner >= 0
            behind = has_left if way == 0 else has_right

            @pl.when(inside)
            def _(way=way, owner=owner, behind=behind):
                held = (right_ref, left_ref)[way]
                place = rows(owner, chunk)

                @pl.when(behind)
                def _():
                    sum_copy(way, owner, chunk).wait_recv()
                    held[place] = (
                        held[place].astype(jnp.float32) + first_ref[place].astype(jnp.float32)
                    ).astype(held.dtype)

                @pl.when(jnp.logical_not(behind))
                def _():
                    held[place] = first_ref[place].astype(held.dtype)

                sum_copy(way, owner, chunk).start()

    def middle_step(chunk):
        place = rows(me, chunk)
        if summed:
            for way, behind in ((0, has_left), (1, has_right)):
                held = (right_ref, left_ref)[way]

                @pl.when(behind)
                def _(way=way):
                    sum_copy(way, me, chunk).wait_recv()

                @pl.when(jnp.logical_not(behind))
                def _(held=held):
                    held[place] = jnp.zeros((part, held.shape[1]), held.dtype)

            total = first_ref[place].astype(jnp.float32) + (
                right_ref[place].astype(jnp.float32) + left_ref[place].astype(jnp.float32)
            )
        else:
            total = first_ref[mine(chunk)]
        result = middle(total, mine(chunk), ins, outs, chunk)
        if spread:
            outs[0][place] = result.astype(outs[0].dtype)

            @pl.when(has_right)
            def _():
                spread_copy(0, me, chunk).start()

            @pl.when(has_left)
            def _():
                spread_copy(1, me, chunk).start()

    def pass_step(distance, chunk):
        @pl.when(me - distance >= 0)
        def _():
            spread_copy(0, me - distance, chunk).wait_recv()

            @pl.when(has_right)
            def _():
                spread_copy(0, me - distance, chunk).start()

        @pl.when(me + distance < size)
        def _():
            spread_copy(1, me + distance, chunk).wait_recv()

            @pl.when(has_left)
            def _():
                spread_copy(1, me + distance, chunk).start()

    def at(step, lag, action):
        chunk = step - lag

        @pl.when((chunk >= 0) & (chunk < steps))
        def _():
            action(chunk)

    lag = size - 1 if summed else 0

    def step_body(step, carry):
        if summed:
            for distance in range(size - 1, 0, -1):
                at(step, size - 1 - distance, functools.partial(sum_step, distance))
        at(step, lag, middle_step)
        if spread:
            for distance in range(1, size):
                at(step, lag + distance, functools.partial(pass_step, distance))
        return carry

    lax.fori_loop(0, steps + lag + (size - 1 if spread else 0), step_body, 0)

    def drain(chunk, carry):
        for distance in range(size):
            if summed and distance > 0:

                @pl.when(me + distance < size)
                def _(distance=distance):
                    sum_copy(0, me + distance, chunk).wait_send()

                @pl.when(me - distance >= 0)
                def _(distance=distance):
                    sum_copy(1, me - distance, chunk).wait_send()

            if spread:

                @pl.when((me - distance >= 0) & has_right)
                def _(distance=distance):
                    spread_copy(0, me - distance, chunk).wait_send()

                @pl.when((me + distance < size) & has_left)
                def _(distance=distance):
                    spread_copy(1, me + distance, chunk).wait_send()

        return carry

    lax.fori_loop(0, steps, drain, 0)


def on_line(size, number, summed, spread, middle, first, ins, out_shapes, steps=STEPS):
    width = first.shape[1]
    all_rows = first.shape[0] if summed else first.shape[0] * size
    scratch = []
    if summed:
        scratch += [
            pltpu.VMEM((all_rows, width), jnp.bfloat16),
            pltpu.VMEM((all_rows, width), jnp.bfloat16),
            pltpu.SemaphoreType.DMA((2, size, steps)),
            pltpu.SemaphoreType.DMA((2, size, steps)),
        ]
    if spread:
        scratch += [
            pltpu.SemaphoreType.DMA((2, size, steps)),
            pltpu.SemaphoreType.DMA((size, steps)),
        ]
        out_shapes = [jax.ShapeDtypeStruct((all_rows, width), jnp.bfloat16)] + list(out_shapes)
    whole = pl.BlockSpec(memory_space=pltpu.VMEM)
    return pl.pallas_call(
        functools.partial(
            line_kernel, size, steps, summed, spread, middle, 1 + len(ins), len(out_shapes)
        ),
        out_shape=out_shapes,
        in_specs=[whole] * (1 + len(ins)),
        out_specs=[whole] * len(out_shapes),
        scratch_shapes=scratch,
        compiler_params=pltpu.CompilerParams(
            collective_id=number, has_side_effects=True, vmem_limit_bytes=40 * 1024 * 1024
        ),
        cost_estimate=pl.CostEstimate(
            flops=LINE_COST * (int(summed) + int(spread)) * all_rows * width,
            bytes_accessed=4 * all_rows * width,
            transcendentals=0,
        ),
    )(first, *ins)


def low(shape):
    return jax.ShapeDtypeStruct(shape, jnp.bfloat16)


def full(shape):
    return jax.ShapeDtypeStruct(shape, jnp.float32)


def middle_gather(total, place, ins, outs, chunk):
    return total


def middle_sum(total, place, ins, outs, chunk):
    outs[0][place] = total


def middle_hidden(branch, place, ins, outs, chunk):
    tokens_ref, gain_ref = ins
    _, branch_ref, hidden_ref = outs
    hidden = tokens_ref[place].astype(jnp.float32) + branch * rms_scale(branch) * gain_ref[...]
    branch_ref[place] = branch
    hidden_ref[place] = hidden
    return hidden


def add_row(gain_ref, values, chunk):
    row = jnp.sum(values, axis=0, keepdims=True)

    @pl.when(chunk == 0)
    def _():
        gain_ref[...] = row

    @pl.when(chunk > 0)
    def _():
        gain_ref[...] += row


def middle_output(branch, place, ins, outs, chunk):
    hidden_ref, cotangent_ref, gain_ref = ins
    _, output_ref, part_ref = outs
    scale = rms_scale(branch)
    scaled = branch * scale
    cotangent = cotangent_ref[place]
    output_ref[place] = hidden_ref[place] + scaled * gain_ref[...]
    add_row(part_ref, cotangent * scaled, chunk)
    return norm_back(branch, scale, gain_ref[...], cotangent)


def middle_branch(total, place, ins, outs, chunk):
    cotangent_ref, branch_ref, gain_ref = ins
    _, grad_ref, part_ref = outs
    branch = branch_ref[place]
    scale = rms_scale(branch)
    grad_hidden = cotangent_ref[place] + total
    grad_ref[place] = grad_hidden
    add_row(part_ref, grad_hidden * branch * scale, chunk)
    return norm_back(branch, scale, gain_ref[...], grad_hidden)


def on_device(
    dp_size,
    tensor_size,
    tokens,
    query_weight,
    key_weight,
    value_weight,
    query_gain,
    key_gain,
    out_weight,
    attn_gain,
    gate_weight,
    up_weight,
    down_weight,
    mlp_gain,
    cotangent,
):
    model_width = tokens.shape[1]
    query_flat = query_gain.reshape(-1)
    key_flat = key_gain.reshape(-1)
    attn_row, mlp_row = attn_gain[None, :], mlp_gain[None, :]
    own_rows = tokens.shape
    on = functools.partial(on_line, tensor_size)
    (gathered,) = on(0, False, True, middle_gather, tokens, (), ())
    row_total = gathered.shape[0]
    head_dim = query_gain.shape[1]
    query_row, key_row = query_flat[None, :], key_flat[None, :]
    cosine_half, sine_half = rope_tables(L, head_dim // 2)
    cosine_table = jnp.concatenate([cosine_half, cosine_half], axis=1)
    sine_table = jnp.concatenate([-sine_half, sine_half], axis=1)
    query_proj = matmul(gathered, query_weight)
    key_proj = matmul(gathered, key_weight)
    value_proj = matmul(gathered, value_weight).astype(jnp.bfloat16)
    query_square, key_square = lax.psum(
        (jnp.sum(query_proj * query_proj, axis=-1), jnp.sum(key_proj * key_proj, axis=-1)), "tensor"
    )
    query_scale = lax.rsqrt(query_square / model_width + rms_eps)[:, None]
    key_scale = lax.rsqrt(key_square / model_width + rms_eps)[:, None]
    attended, query_rot, key_rot = head_call(
        attend_kernel,
        (
            query_proj,
            key_proj,
            value_proj,
            query_scale,
            key_scale,
            query_row,
            key_row,
            cosine_table,
            sine_table,
        ),
        [low(value_proj.shape)] * 3,
        head_dim,
    )
    hidden_rows, attn_branch, hidden = on(
        1,
        True,
        True,
        middle_hidden,
        matmul(attended, out_weight),
        (tokens, attn_row),
        (full(own_rows), full(own_rows)),
    )
    gate_proj = matmul(hidden_rows, gate_weight)
    up_proj = matmul(hidden_rows, up_weight)
    sigmoid_gate = jax.nn.sigmoid(gate_proj)
    swish_gate = gate_proj * sigmoid_gate
    activation = (swish_gate * up_proj).astype(jnp.bfloat16)
    grad_mlp_rows, output, part_mlp_gain = on(
        2,
        True,
        True,
        middle_output,
        matmul(activation, down_weight),
        (hidden, cotangent, mlp_row),
        (full(own_rows), full(mlp_row.shape)),
    )
    grad_act = matmul_nt(grad_mlp_rows, down_weight)
    grad_gate = (
        grad_act * up_proj * sigmoid_gate * (1.0 + gate_proj * (1.0 - sigmoid_gate))
    ).astype(jnp.bfloat16)
    grad_up = (grad_act * swish_gate).astype(jnp.bfloat16)
    summed_down = reduce_product(
        lambda part: matmul_tn(activation, part), *by_owner(grad_mlp_rows, dp_size), 1, dp_size
    )
    hidden_parts = by_owner(hidden_rows, dp_size)
    summed_gate = reduce_product(
        lambda part: matmul_tn(part, grad_gate), *hidden_parts, 0, dp_size
    )
    summed_up = reduce_product(lambda part: matmul_tn(part, grad_up), *hidden_parts, 0, dp_size)
    grad_branch_rows, grad_hidden, part_attn_gain = on(
        3,
        True,
        True,
        middle_branch,
        matmul_nt(grad_gate, gate_weight) + matmul_nt(grad_up, up_weight),
        (cotangent, attn_branch, attn_row),
        (full(own_rows), full(attn_row.shape)),
    )
    grad_attended = matmul_nt(grad_branch_rows, out_weight).astype(jnp.bfloat16)
    summed_out = reduce_product(
        lambda part: matmul_tn(attended, part), *by_owner(grad_branch_rows, dp_size), 1, dp_size
    )
    row_total = gathered.shape[0]
    terms_shape = (row_total // L, 1, query_flat.shape[0])
    query_weighted, key_weighted, grad_value, query_part, key_part, query_terms, key_terms = head_call(
        attend_back_kernel,
        (
            grad_attended,
            query_rot,
            key_rot,
            value_proj,
            query_proj,
            key_proj,
            query_scale,
            key_scale,
            query_row,
            key_row,
            cosine_table,
            sine_table,
        ),
        [
            full(query_proj.shape),
            full(query_proj.shape),
            low(query_proj.shape),
            full((row_total, 1)),
            full((row_total, 1)),
            full(terms_shape),
            full(terms_shape),
        ],
        head_dim,
    )
    term_query_gain = jnp.sum(query_terms, axis=0).reshape(query_gain.shape)
    term_key_gain = jnp.sum(key_terms, axis=0).reshape(key_gain.shape)
    query_inner, key_inner = lax.psum((query_part[:, 0], key_part[:, 0]), "tensor")
    grad_query = (
        query_scale
        * (
            query_weighted
            - query_proj * query_scale * query_scale * (query_inner / model_width)[:, None]
        )
    ).astype(jnp.bfloat16)
    grad_key = (
        key_scale
        * (key_weighted - key_proj * key_scale * key_scale * (key_inner / model_width)[:, None])
    ).astype(jnp.bfloat16)
    token_parts = by_owner(gathered, dp_size)
    width = grad_query.shape[1]
    grad_three = jnp.concatenate([grad_query, grad_key, grad_value], axis=1)
    summed_three = reduce_product(
        lambda part: matmul_tn(part, grad_three), *token_parts, 0, dp_size
    )
    summed_query, summed_key, summed_value = (
        summed_three[:, :width],
        summed_three[:, width : 2 * width],
        summed_three[:, 2 * width :],
    )
    (input_sum,) = on(
        4,
        True,
        False,
        middle_sum,
        matmul_nt(grad_query, query_weight)
        + matmul_nt(grad_key, key_weight)
        + matmul_nt(grad_value, value_weight),
        (),
        (full(own_rows),),
    )
    input_grad = grad_hidden + input_sum
    place = lax.axis_index("dp")
    summed_gains = add_all(
        add_all(jnp.concatenate([part_attn_gain, part_mlp_gain]), "tensor", tensor_size), "dp", dp_size
    )
    summed_gains = own_part(
        summed_gains,
        1,
        place * tensor_size + lax.axis_index("tensor"),
        dp_size * tensor_size,
    )
    summed_attn_gain, summed_mlp_gain = summed_gains[0], summed_gains[1]
    head_gains = own_part(
        add_all(jnp.stack([term_query_gain, term_key_gain]), "dp", dp_size), 2, place, dp_size
    )
    summed_query_gain, summed_key_gain = head_gains[0], head_gains[1]
    return (
        output,
        input_grad,
        summed_query,
        summed_key,
        summed_value,
        summed_query_gain,
        summed_key_gain,
        summed_out,
        summed_attn_gain,
        summed_gate,
        summed_up,
        summed_down,
        summed_mlp_gain,
    )


def solution(mesh):
    placed = (
        P(("dp", "tensor"), None),
        P(None, "tensor"),
        P(None, "tensor"),
        P(None, "tensor"),
        P("tensor", None),
        P("tensor", None),
        P("tensor", None),
        P(),
        P(None, "tensor"),
        P(None, "tensor"),
        P("tensor", None),
        P(),
        P(("dp", "tensor"), None),
    )
    return jax.shard_map(
        functools.partial(on_device, mesh.shape["dp"], mesh.shape["tensor"]),
        mesh=mesh,
        in_specs=placed,
        out_specs=(
            P(("dp", "tensor"), None),
            P(("dp", "tensor"), None),
            P("dp", "tensor"),
            P("dp", "tensor"),
            P("dp", "tensor"),
            P("tensor", "dp"),
            P("tensor", "dp"),
            P("tensor", "dp"),
            P(("dp", "tensor")),
            P("dp", "tensor"),
            P("dp", "tensor"),
            P("tensor", "dp"),
            P(("dp", "tensor")),
        ),
        check_vma=False,
    )
```

time: 643 us -> 598 us (0.930)
  Pallas kernels: 0 us -> 287 us
  waiting for transfers between devices: 315 us -> 89.6 us
  local copies, waits for them, and re-layouts: 60.5 us -> 24.8 us
  matrix products: 145 us -> 116 us
  other arithmetic: 45.1 us -> 22.8 us
  between operations: 16 us -> 2.1 us
    pallas_call x0 -> x11, Pallas kernels: none -> 287 us  [the longest x5 250 us: on_line(): pl.pallas_call(functools.partial(line_kernel, size, steps, summed, spread...]
    all_gather x4 -> x0, waiting for transfers between devices: 133 us -> none  [the longest x1 48.7 us: on_device(): gathered = lax.all_gather(tokens, 'tensor', axis=0, tiled=True)]
    reduce_scatter x4 -> x0, waiting for transfers between devices: 95 us -> none  [scatter_low(): lax.psum_scatter(values.astype(jnp.bfloat16), 'tensor', scatter_dimension...]
    ppermute x25, waiting for transfers between devices: 57.4 us -> 83.3 us  [exchange(): return lax.ppermute(values, 'dp', swap_pairs(size, step))]
    ppermute x8, waiting for transfers between devices: 28.6 us -> 6.29 us  [add_all(): values = values + lax.ppermute(values, name, swap_pairs(size, step))]
    dot_general x6 -> x0, matrix products: 20.7 us -> none  [the longest x1 6.01 us: attend_back(): jnp.einsum('shqk,skhd->sqhd', grad_scores, keys_all, preferred_element_ty...]
    unnamed x186 -> x110, local copies, waits for them, and re-layouts: 30.4 us -> 11 us
    dot_general x7, matrix products: 40.3 us -> 31.1 us  [matmul(): return jnp.dot(left, right, preferred_element_type=jnp.float32)]
  transfers between devices with their start and end apart: 41 -> 33, of which waited for: 20 -> 17; matrix products, arithmetic and copies ran while one was open for 17% -> 13% of each run, Pallas kernels for 0% -> 8%
where the time goes in v2:
time: 598 us; the launch traced here: 591 us
  Pallas kernels  287 us (48%)
  matrix products  116 us (19%)
  waiting for transfers between devices  89.6 us (15%)
  starting transfers between devices  28 us (5%)
  local copies, waits for them, and re-layouts  24.8 us (4%)
  other arithmetic  22.8 us (4%)
  blocking collectives  20.9 us (3%)
    pallas_call x5, Pallas kernels, on_line(): pl.pallas_call(functools.partial(line_kernel, size, steps, summed, spread...  250 us
    ppermute x25, waiting for transfers between devices, exchange(): return lax.ppermute(values, 'dp', swap_pairs(size, step))  83.3 us
    dot_general x10, matrix products, matmul_tn(): lax.dot_general(left, right, (((0,), (0,)), ((), ())), preferred_element_...  42.8 us
    dot_general x7, matrix products, matmul_nt(): lax.dot_general(left, right, (((1,), (1,)), ((), ())), preferred_element_...  42.2 us
    dot_general x7, matrix products, matmul(): return jnp.dot(left, right, preferred_element_type=jnp.float32)  31.1 us
    pallas_call x2, Pallas kernels, head_call(): pl.pallas_call(kernel, grid=grid, out_shape=out_shapes, in_specs=[spec(me...  23.2 us
    ppermute x25, starting transfers between devices, exchange(): return lax.ppermute(values, 'dp', swap_pairs(size, step))  21.9 us
    pallas_call x4, Pallas kernels, pick_blocks(): pl.pallas_call(functools.partial(pick_kernel, part), in_specs=[pl.BlockSp...  13.8 us
  transfers between devices with their start and end apart: 33, of which 17 were waited for; matrix products, arithmetic and copies ran while one was open for 13% of the time, Pallas kernels for 8%

profile of v2, /device:TPU:0, one launch (start us, length us, event | category | flops | bytes accessed | tf_op | source)
XLA Modules:
  0.0 591.5 jit_solution(9571421462471355152)
XLA Ops:
  1.9 40.2 %shard_map.228.source_ref = bf16[512,2048]{1,0:T(8,128)(2,1)S(1)} custom-call(bf16[128,2048]{1,0:T(8,128)(2,1)S(1)} %copy-done.9), custom_call_target="tpu_custom_call" | custom-call | flops 3145728000 | bytes 4194304 | tf_op jit(solution)/shard_map/pallas_call | solution.py:491
  44.7 3.5 multiply_reduce_fusion
  49.6 4.3 convolution_convert_fusion.6.value_ref
  53.8 10.2 %all-reduce.1 = (f32[512]{0:T(512)S(1)}, f32[512]{0:T(512)S(1)}) all-reduce(f32[512]{0:T(512)S(1)} %get-tuple-element.113, f32[512]{0:T(512)S(1)} %get-tuple-element.115), channel_id=1, replica_groups=mesh['dp'=8,'tensor'=4] {'tensor'}, use_global_device_ids=true, to_apply=%region_1.2 | all-reduce | flops 1024 | bytes 8192 | tf_op jit(solution)/shard_map/psum | solution.py:602
  67.2 8.8 %shard_map.229 = (bf16[512,512]{1,0:T(8,128)(2,1)}, bf16[512,512]{1,0:T(8,128)(2,1)}, bf16[512,512]{1,0:T(8,128)(2,1)}) custom-call(f32[512,512]{1,0:T(8,128)} %copy.34.query_ref, f32[512,512]{1,0:T(8,128)} %copy.35.key_ref, bf16[512,512]{1,0:T(8,128)(2,1)} %convolution_convert_fusion.6.value_ref, f32[512,1]{1,0:T(8,128)} %copy.36.query_scale_ref, ...), custom_call_target="tpu_custom_call" | custom-call | flops 536870912 | bytes 4194304 | tf_op jit(solution)/shard_map/pallas_call | solution.py:171
  76.1 3.1 fusion.44.refs_0_
  79.2 57.2 %shard_map.230 = (bf16[512,2048]{1,0:T(8,128)(2,1)S(1)}, f32[128,2048]{1,0:T(8,128)S(1)}, f32[128,2048]{1,0:T(8,128)S(1)}) custom-call(f32[512,2048]{1,0:T(8,128)S(1)} %fusion.44.refs_0_, bf16[128,2048]{1,0:T(8,128)(2,1)S(1)} %copy-done.10, f32[1,2048]{1,0:T(1,128)S(1)} %bitcast.69), custom_call_target="tpu_custom_call" | custom-call | flops 6291456000 | bytes 4194304 | tf_op jit(solution)/shard_map/pallas_call | solution.py:491
  136.4 8.0 %fusion.45 = f32[512,2048]{1,0:T(8,128)S(1)} fusion(bf16[512,2048]{1,0:T(8,128)(2,1)S(1)} %get-tuple-element.33.source_ref, bf16[2048,2048]{1,0:T(8,128)(2,1)} %param.21), kind=kOutput, calls=%fused_computation.115 | convolution fusion | flops 4294967296 | bytes 14680064 | tf_op jit(solution)/shard_map/dot_general | solution.py:19
  144.5 6.3 %multiply_convert_fusion.2 = (bf16[512,2048]{1,0:T(8,128)(2,1)S(1)}, f32[512,2048]{1,0:T(8,128)}) fusion(f32[512,2048]{1,0:T(8,128)S(1)} %fusion.45, bf16[512,2048]{1,0:T(8,128)(2,1)S(1)} %get-tuple-element.33.source_ref, bf16[2048,2048]{1,0:T(8,128)(2,1)S(1)} %bitcast.86), kind=kOutput, calls=%fused_computation.7 | convolution fusion | flops 4301258752 | bytes 20971520 | tf_op jit(solution)/shard_map/dot_general | solution.py:19
  150.9 4.6 fusion.46.refs_0_
  155.5 59.3 %shard_map.231 = (bf16[512,2048]{1,0:T(8,128)(2,1)S(1)}, f32[128,2048]{1,0:T(8,128)S(1)}, f32[1,2048]{1,0:T(1,128)S(1)}) custom-call(f32[512,2048]{1,0:T(8,128)S(1)} %fusion.46.refs_0_, f32[128,2048]{1,0:T(8,128)S(1)} %get-tuple-element.34.refs_1_, f32[128,2048]{1,0:T(8,128)S(1)} %copy-done.8, f32[1,2048]{1,0:T(1,128)S(1)} %bitcast.68), custom_call_target="tpu_custom_call" | custom-call | flops 6291456000 | bytes 4194304 | tf_op jit(solution)/shard_map/pallas_call | solution.py:491
  215.8 12.4 %multiply_convert_fusion = (bf16[512,2048]{1,0:T(8,128)(2,1)}, bf16[512,2048]{1,0:T(8,128)(2,1)S(1)}) fusion(f32[512,2048]{1,0:T(8,128)} %copy-done.49, f32[512,2048]{1,0:T(8,128)} %get-tuple-element.118, bf16[512,2048]{1,0:T(8,128)(2,1)S(1)} %get-tuple-element.36.source_ref, bf16[2048,2048]{1,0:T(8,128)(2,1)} %param.23), kind=kOutput, calls=%fused_computation.5 | convolution fusion | flops 4308598784 | bytes 23068672 | tf_op jit(solution)/shard_map/dot_general | solution.py:23
  228.1 8.0 %fusion.47 = f32[512,2048]{1,0:T(8,128)S(1)} fusion(bf16[512,2048]{1,0:T(8,128)(2,1)S(1)} %get-tuple-element.88, bf16[2048,2048]{1,0:T(8,128)(2,1)} %param.21), kind=kOutput, calls=%fused_computation.117 | convolution fusion | flops 4294967296 | bytes 14680064 | tf_op jit(solution)/shard_map/dot_general | solution.py:23
  236.1 7.3 %convolution_add_fusion.refs_0_ = f32[512,2048]{1,0:T(8,128)S(1)} fusion(f32[512,2048]{1,0:T(8,128)S(1)} %fusion.47, bf16[512,2048]{1,0:T(8,128)(2,1)S(1)} %copy-done.37, bf16[2048,2048]{1,0:T(8,128)(2,1)} %param.22), kind=kOutput, calls=%fused_computation.14 | convolution fusion | flops 4296015872 | bytes 18874368 | tf_op jit(solution)/shard_map/dot_general | solution.py:23
  243.4 53.8 %shard_map.232 = (bf16[512,2048]{1,0:T(8,128)(2,1)S(1)}, f32[128,2048]{1,0:T(8,128)S(1)}, f32[1,2048]{1,0:T(1,128)S(1)}) custom-call(f32[512,2048]{1,0:T(8,128)S(1)} %convolution_add_fusion.refs_0_, f32[128,2048]{1,0:T(8,128)S(1)} %copy-done.8, f32[128,2048]{1,0:T(8,128)S(1)} %copy-done.14, f32[1,2048]{1,0:T(1,128)S(1)} %bitcast.70), custom_call_target="tpu_custom_call" | custom-call | flops 6291456000 | bytes 4194304 | tf_op jit(solution)/shard_map/pallas_call | solution.py:491
  297.2 2.2 convolution_convert_fusion.5.upstream_ref
  299.4 14.4 %shard_map.233 = (f32[512,512]{1,0:T(8,128)}, f32[512,512]{1,0:T(8,128)}, bf16[512,512]{1,0:T(8,128)(2,1)}, f32[512,1]{1,0:T(8,128)}, f32[512,1]{1,0:T(8,128)}, ...) custom-call(bf16[512,512]{1,0:T(8,128)(2,1)} %convolution_convert_fusion.5.upstream_ref, ...), custom_call_target="tpu_custom_call" | custom-call | flops 536870912 | bytes 4194304 | tf_op jit(solution)/shard_map/pallas_call | solution.py:171
  316.0 10.7 %all-reduce = (f32[512]{0:T(512)S(1)}, f32[512]{0:T(512)S(1)}) all-reduce(f32[512]{0:T(512)S(1)} %reduce.2, f32[512]{0:T(512)S(1)} %reduce.3), channel_id=1, replica_groups=mesh['dp'=8,'tensor'=4] {'tensor'}, use_global_device_ids=true, to_apply=%region_4.5 | all-reduce | flops 1024 | bytes 8192 | tf_op jit(solution)/shard_map/psum | solution.py:703
  327.4 3.5 shard_map.235
  333.9 3.5 convolution_convert_fusion.3
  338.1 3.5 shard_map.236
  341.5 3.1 convolution_convert_fusion.4
  344.8 3.4 shard_map.237
  348.2 6.4 %convolution_convert_fusion.2 = bf16[1024,2048]{1,0:T(8,128)(2,1)} fusion(bf16[512,2048]{1,0:T(8,128)(2,1)} %copy-done.40, bf16[512,2048]{1,0:T(8,128)(2,1)} %shard_map.237), kind=kOutput, calls=%fused_computation.12 | convolution fusion | flops 2149580800 | bytes 7340032 | tf_op jit(solution)/shard_map/dot_general | solution.py:29
  355.2 3.2 fusion.48
  358.4 3.3 fusion.49
  361.7 4.4 convolution_convert_fusion.1
  366.2 3.4 shard_map.238
  369.6 5.8 add_add_fusion.refs_0_
  375.5 4.4 convolution_convert_fusion
  386.5 39.9 %shard_map.234 = f32[128,2048]{1,0:T(8,128)S(1)} custom-call(f32[512,2048]{1,0:T(8,128)S(1)} %add_add_fusion.refs_0_), custom_call_target="tpu_custom_call" | custom-call | flops 3145728000 | bytes 4194304 | tf_op jit(solution)/shard_map/pallas_call | solution.py:491
  427.9 3.3 collective-permute-done.16
  432.7 2.4 fusion.40
  436.9 4.7 collective-permute-done.9
  444.7 3.8 fusion.39
  452.1 14.4 %collective-permute-done.3 = bf16[256,1536]{1,0:T(8,128)(2,1)S(1)} collective-permute-done((bf16[256,1536]{1,0:T(8,128)(2,1)S(1)}, bf16[256,1536]{1,0:T(8,128)(2,1)S(1)}, u32[]{:S(2)}, u32[]{:S(2)}) %collective-permute-start.3) | collective-permute-done | bytes 786464 | tf_op jit(solution)/shard_map/ppermute | solution.py:239
  471.2 4.7 fusion.41
  478.5 2.0 copy-done.19
  481.5 4.7 fusion.42
  487.8 2.0 copy-done.18
  491.3 5.3 fusion.43
  506.8 2.5 slice_add_fusion.5
  510.6 15.8 %collective-permute-done.24 = bf16[256,2048]{1,0:T(8,128)(2,1)} collective-permute-done((bf16[256,2048]{1,0:T(8,128)(2,1)}, bf16[256,2048]{1,0:T(8,128)(2,1)}, u32[]{:S(2)}, u32[]{:S(2)}) %collective-permute-start.24) | collective-permute-done | bytes 1048608 | tf_op jit(solution)/shard_map/ppermute | solution.py:239
  529.3 2.3 slice_add_fusion.3
  534.6 14.2 %collective-permute-done.29 = bf16[2048,256]{0,1:T(8,128)(2,1)S(1)} collective-permute-done((bf16[2048,256]{0,1:T(8,128)(2,1)}, bf16[2048,256]{0,1:T(8,128)(2,1)S(1)}, u32[]{:S(2)}, u32[]{:S(2)}) %collective-permute-start.29) | collective-permute-done | bytes 1048608 | tf_op jit(solution)/shard_map/ppermute | solution.py:239
  553.9 6.1 %collective-permute-done.22 = bf16[128,2048]{1,0:T(8,128)(2,1)S(1)} collective-permute-done((bf16[128,2048]{1,0:T(8,128)(2,1)S(1)}, bf16[128,2048]{1,0:T(8,128)(2,1)S(1)}, u32[]{:S(2)}, u32[]{:S(2)}) %collective-permute-start.22) | collective-permute-done | bytes 524320 | tf_op jit(solution)/shard_map/ppermute | solution.py:239
  563.0 16.4 %collective-permute-done.32 = bf16[2048,128]{0,1:T(8,128)(2,1)S(1)} collective-permute-done((bf16[2048,128]{0,1:T(8,128)(2,1)S(1)}, bf16[2048,128]{0,1:T(8,128)(2,1)S(1)}, u32[]{:S(2)}, u32[]{:S(2)}) %collective-permute-start.32) | collective-permute-done | bytes 524320 | tf_op jit(solution)/shard_map/ppermute | solution.py:239
  579.5 2.8 collective-permute-done.30
  (233 shorter events, 80.0 us)
Async XLA Ops:
  0.6 41.4 %copy-start = (bf16[2048,512]{1,0:T(8,128)(2,1)S(1)}, bf16[2048,512]{1,0:T(8,128)(2,1)}, u32[]{:S(2)}) copy-start(bf16[2048,512]{1,0:T(8,128)(2,1)} %param.14) | copy-start | bytes 6291460
  79.2 65.3 %slice-start.2 = ((s8[8388608]{0:T(1024)(128)(4,1)}), s8[4194304]{0:T(1024)(128)(4,1)S(1)}, s32[]{:S(2)}) async-start(s8[8388608]{0:T(1024)(128)(4,1)} %bitcast.85), calls=%async_computation.2 | async-start | bytes 8388608
  136.4 8.1 %copy-start.4 = (bf16[512,2048]{1,0:T(8,128)(2,1)}, bf16[512,2048]{1,0:T(8,128)(2,1)S(1)}, u32[]{:S(2)}) copy-start(bf16[512,2048]{1,0:T(8,128)(2,1)S(1)} %get-tuple-element.33.source_ref) | copy-start | bytes 6291460
  136.4 8.1 %copy-start.13 = (f32[128,2048]{1,0:T(8,128)}, f32[128,2048]{1,0:T(8,128)S(1)}, u32[]{:S(2)}) copy-start(f32[128,2048]{1,0:T(8,128)S(1)} %get-tuple-element.37.refs_2_) | copy-start | bytes 3145732
  136.4 8.1 %slice-start.3 = ((s8[8388608]{0:T(1024)(128)(4,1)}), s8[4194304]{0:T(1024)(128)(4,1)S(1)}, s32[]{:S(2)}) async-start(s8[8388608]{0:T(1024)(128)(4,1)} %bitcast.85), calls=%async_computation.3 | async-start | bytes 8388608
  136.4 14.4 %slice-start = ((s8[8388608]{0:T(1024)(128)(4,1)}), s8[4194304]{0:T(1024)(128)(4,1)S(1)}, s32[]{:S(2)}) async-start(s8[8388608]{0:T(1024)(128)(4,1)} %bitcast.83), calls=%async_computation | async-start | bytes 8388608
  215.7 12.4 %copy-start.3 = (bf16[512,2048]{1,0:T(8,128)(2,1)}, bf16[512,2048]{1,0:T(8,128)(2,1)S(1)}, u32[]{:S(2)}) copy-start(bf16[512,2048]{1,0:T(8,128)(2,1)S(1)} %get-tuple-element.36.source_ref) | copy-start | bytes 6291460
  228.1 8.0 %copy-start.37 = (bf16[512,2048]{1,0:T(8,128)(2,1)S(1)}, bf16[512,2048]{1,0:T(8,128)(2,1)}, u32[]{:S(2)}) copy-start(bf16[512,2048]{1,0:T(8,128)(2,1)} %get-tuple-element.87) | copy-start | bytes 6291460
  243.4 53.8 %copy-start.42 = (bf16[512,2048]{1,0:T(8,128)(2,1)S(1)}, bf16[512,2048]{1,0:T(8,128)(2,1)}, u32[]{:S(2)}) copy-start(bf16[512,2048]{1,0:T(8,128)(2,1)} %param.19) | copy-start | bytes 6291460
  337.4 106.5 %collective-permute-start = (bf16[1024,1536]{1,0:T(8,128)(2,1)}, bf16[1024,1536]{1,0:T(8,128)(2,1)}, u32[]{:S(2)}, u32[]{:S(2)}) collective-permute-start(bf16[1024,1536]{1,0:T(8,128)(2,1)} %convolution_convert_fusion.3), channel_id=1, source_target_pairs={{0,4},{4,0},{8,12},{12,8},{16,20},{20,16},{24,28},{28,24},{1,5},{5... | collective-permute-start | bytes 9437192 | tf_op jit(solution)/shard_map/ppermute | solution.py:239
  337.5 42.3 %collective-permute-start.5 = (f32[2,4,128]{2,1,0:T(4,128)S(1)}, f32[2,4,128]{2,1,0:T(4,128)S(1)}, u32[]{:S(2)}, u32[]{:S(2)}) collective-permute-start(f32[2,4,128]{2,1,0:T(4,128)S(1)} %pad_maximum_fusion.11), channel_id=1, source_target_pairs={{0,4},{4,0},{8,12},{12,8},{16,20},{20,16},{24,28},{28,24},{1,5},{5... | collective-permute-start | bytes 12296 | tf_op jit(solution)/shard_map/ppermute | solution.py:268
  344.6 88.0 %collective-permute-start.8 = (bf16[512,1024]{1,0:T(8,128)(2,1)}, bf16[512,1024]{1,0:T(8,128)(2,1)}, u32[]{:S(2)}, u32[]{:S(2)}) collective-permute-start(bf16[512,1024]{1,0:T(8,128)(2,1)} %convolution_convert_fusion.4), channel_id=1, source_target_pairs={{0,4},{4,0},{8,12},{12,8},{16,20},{20,16},{24,28},{28,24},{1,5},{5... | collective-permute-start | bytes 3145736 | tf_op jit(solution)/shard_map/ppermute | solution.py:239
  344.7 36.9 %collective-permute-start.13 = (f32[2,2048]{1,0:T(2,128)S(1)}, f32[2,2048]{1,0:T(2,128)S(1)}, u32[]{:S(2)}, u32[]{:S(2)}) collective-permute-start(f32[2,2048]{1,0:T(2,128)S(1)} %pad_maximum_fusion.10), channel_id=1, source_target_pairs={{0,1},{1,0},{2,3},{3,2},{4,5},{5,4},{6,7},{7,6},{8,9},{9,8},{10,11... | collective-permute-start | bytes 49160 | tf_op jit(solution)/shard_map/ppermute | solution.py:268
  354.7 116.6 %collective-permute-start.18 = (bf16[1024,2048]{1,0:T(8,128)(2,1)}, bf16[1024,2048]{1,0:T(8,128)(2,1)}, u32[]{:S(2)}, u32[]{:S(2)}) collective-permute-start(bf16[1024,2048]{1,0:T(8,128)(2,1)} %convolution_convert_fusion.2), channel_id=1, source_target_pairs={{0,4},{4,0},{8,12},{12,8},{16,20},{20,16},{24,28},{28,24},{1,5},{5... | collective-permute-start | bytes 12582920 | tf_op jit(solution)/shard_map/ppermute | solution.py:239
  379.9 3.7 collective-permute-start.6
  381.7 4.7 collective-permute-start.14
  383.5 44.3 %collective-permute-start.7 = (f32[2,4,128]{2,1,0:T(4,128)S(1)}, f32[2,4,128]{2,1,0:T(4,128)S(1)}, u32[]{:S(2)}, u32[]{:S(2)}) collective-permute-start(f32[2,4,128]{2,1,0:T(4,128)S(1)} %fusion.87), channel_id=1, source_target_pairs={{0,16},{4,20},{8,24},{12,28},{16,0},{20,4},{24,8},{28,12},{1,17},{... | collective-permute-start | bytes 12296 | tf_op jit(solution)/shard_map/ppermute | solution.py:268
  386.4 41.1 %collective-permute-start.15 = (f32[2,2048]{1,0:T(2,128)S(1)}, f32[2,2048]{1,0:T(2,128)S(1)}, u32[]{:S(2)}, u32[]{:S(2)}) collective-permute-start(f32[2,2048]{1,0:T(2,128)S(1)} %fusion.86), channel_id=1, source_target_pairs={{0,4},{4,0},{8,12},{12,8},{16,20},{20,16},{24,28},{28,24},{1,5},{5... | collective-permute-start | bytes 49160 | tf_op jit(solution)/shard_map/ppermute | solution.py:268
  427.5 3.8 collective-permute-start.16
  431.3 5.6 collective-permute-start.17
  435.1 9.6 %copy-start.22 = (bf16[512,512]{1,0:T(8,128)(2,1)S(1)}, bf16[512,512]{1,0:T(8,128)(2,1)}, u32[]{:S(2)}) copy-start(bf16[512,512]{1,0:T(8,128)(2,1)} %copy-done.20) | copy-start | bytes 1572868
  435.1 9.6 %copy-start.25 = (bf16[512,512]{1,0:T(8,128)(2,1)S(1)}, bf16[512,512]{1,0:T(8,128)(2,1)}, u32[]{:S(2)}) copy-start(bf16[512,512]{1,0:T(8,128)(2,1)} %copy-done.23) | copy-start | bytes 1572868
  435.1 9.6 %copy-start.30 = (bf16[512,2048]{1,0:T(8,128)(2,1)S(1)}, bf16[512,2048]{1,0:T(8,128)(2,1)}, u32[]{:S(2)}) copy-start(bf16[512,2048]{1,0:T(8,128)(2,1)} %shard_map.235) | copy-start | bytes 6291460
  435.1 9.6 %copy-start.45 = (bf16[512,512]{1,0:T(8,128)(2,1)S(1)}, bf16[512,512]{1,0:T(8,128)(2,1)}, u32[]{:S(2)}) copy-start(bf16[512,512]{1,0:T(8,128)(2,1)} %get-tuple-element.46) | copy-start | bytes 1572868
  435.2 6.4 %collective-permute-start.9 = (bf16[512,256]{1,0:T(8,128)(2,1)S(1)}, bf16[512,256]{1,0:T(8,128)(2,1)S(1)}, u32[]{:S(2)}, u32[]{:S(2)}) collective-permute-start(bf16[512,256]{1,0:T(8,128)(2,1)S(1)} %get-tuple-element.104), channel_id=1, source_target_pairs={{0,8},{4,12},{8,0},{12,4},{16,24},{20,28},{24,16},{28,20},{1,9},{5... | collective-permute-start | bytes 786440 | tf_op jit(solution)/shard_map/ppermute | solution.py:239
  435.8 6.4 %collective-permute-start.11 = (bf16[512,256]{1,0:T(8,128)(2,1)S(1)}, bf16[512,256]{1,0:T(8,128)(2,1)S(1)}, u32[]{:S(2)}, u32[]{:S(2)}) collective-permute-start(bf16[512,256]{1,0:T(8,128)(2,1)S(1)} %get-tuple-element.105), channel_id=1, source_target_pairs={{0,16},{4,20},{8,24},{12,28},{16,0},{20,4},{24,8},{28,12},{1,17},{... | collective-permute-start | bytes 786440 | tf_op jit(solution)/shard_map/ppermute | solution.py:239
  436.9 41.6 %collective-permute-start.23 = (bf16[1024,2048]{1,0:T(8,128)(2,1)}, bf16[1024,2048]{1,0:T(8,128)(2,1)S(1)}, u32[]{:S(2)}, u32[]{:S(2)}) collective-permute-start(bf16[1024,2048]{1,0:T(8,128)(2,1)} %convolution_convert_fusion.1), channel_id=1, source_target_pairs={{0,4},{4,0},{8,12},{12,8},{16,20},{20,16},{24,28},{28,24},{1,5},{5... | collective-permute-start | bytes 12582920 | tf_op jit(solution)/shard_map/ppermute | solution.py:239
  441.6 46.2 %collective-permute-start.28 = (bf16[2048,1024]{0,1:T(8,128)(2,1)}, bf16[2048,1024]{0,1:T(8,128)(2,1)S(1)}, u32[]{:S(2)}, u32[]{:S(2)}) collective-permute-start(bf16[2048,1024]{0,1:T(8,128)(2,1)} %convolution_convert_fusion), channel_id=1, source_target_pairs={{0,4},{4,0},{8,12},{12,8},{16,20},{20,16},{24,28},{28,24},{1,5},{5... | collective-permute-start | bytes 12582920 | tf_op jit(solution)/shard_map/ppermute | solution.py:239
  442.4 6.3 %collective-permute-start.12 = (bf16[512,128]{1,0:T(8,128)(2,1)S(1)}, bf16[512,128]{1,0:T(8,128)(2,1)S(1)}, u32[]{:S(2)}, u32[]{:S(2)}) collective-permute-start(bf16[512,128]{1,0:T(8,128)(2,1)S(1)} %slice.408), channel_id=1, source_target_pairs={{0,8},{4,12},{8,0},{12,4},{16,24},{20,28},{24,16},{28,20},{1,9},{5... | collective-permute-start | bytes 393224 | tf_op jit(solution)/shard_map/ppermute | solution.py:239
  444.0 6.1 %collective-permute-start.10 = (bf16[512,128]{1,0:T(8,128)(2,1)S(1)}, bf16[512,128]{1,0:T(8,128)(2,1)S(1)}, u32[]{:S(2)}, u32[]{:S(2)}) collective-permute-start(bf16[512,128]{1,0:T(8,128)(2,1)S(1)} %slice.409), channel_id=1, source_target_pairs={{0,16},{4,20},{8,24},{12,28},{16,0},{20,4},{24,8},{28,12},{1,17},{... | collective-permute-start | bytes 393224 | tf_op jit(solution)/shard_map/ppermute | solution.py:239
  448.7 17.8 %collective-permute-start.3 = (bf16[256,1536]{1,0:T(8,128)(2,1)S(1)}, bf16[256,1536]{1,0:T(8,128)(2,1)S(1)}, u32[]{:S(2)}, u32[]{:S(2)}) collective-permute-start(bf16[256,1536]{1,0:T(8,128)(2,1)S(1)} %get-tuple-element.97), channel_id=1, source_target_pairs={{0,16},{4,20},{8,24},{12,28},{16,0},{20,4},{24,8},{28,12},{1,17},{... | collective-permute-start | bytes 2359304 | tf_op jit(solution)/shard_map/ppermute | solution.py:239
  450.1 17.7 %collective-permute-start.1 = (bf16[256,1536]{1,0:T(8,128)(2,1)S(1)}, bf16[256,1536]{1,0:T(8,128)(2,1)S(1)}, u32[]{:S(2)}, u32[]{:S(2)}) collective-permute-start(bf16[256,1536]{1,0:T(8,128)(2,1)S(1)} %get-tuple-element.98), channel_id=1, source_target_pairs={{0,8},{4,12},{8,0},{12,4},{16,24},{20,28},{24,16},{28,20},{1,9},{5... | collective-permute-start | bytes 2359304 | tf_op jit(solution)/shard_map/ppermute | solution.py:239
  469.0 29.1 %collective-permute-start.4 = (bf16[128,1536]{1,0:T(8,128)(2,1)}, bf16[128,1536]{1,0:T(8,128)(2,1)}, u32[]{:S(2)}, u32[]{:S(2)}) collective-permute-start(bf16[128,1536]{1,0:T(8,128)(2,1)} %slice.406), channel_id=1, source_target_pairs={{0,8},{4,12},{8,0},{12,4},{16,24},{20,28},{24,16},{28,20},{1,9},{5... | collective-permute-start | bytes 1179656 | tf_op jit(solution)/shard_map/ppermute | solution.py:239
  470.5 29.4 %collective-permute-start.2 = (bf16[128,1536]{1,0:T(8,128)(2,1)S(1)}, bf16[128,1536]{1,0:T(8,128)(2,1)}, u32[]{:S(2)}, u32[]{:S(2)}) collective-permute-start(bf16[128,1536]{1,0:T(8,128)(2,1)S(1)} %slice.407), channel_id=1, source_target_pairs={{0,16},{4,20},{8,24},{12,28},{16,0},{20,4},{24,8},{28,12},{1,17},{... | collective-permute-start | bytes 1179656 | tf_op jit(solution)/shard_map/ppermute | solution.py:239
  477.5 26.3 %collective-permute-start.19 = (bf16[256,2048]{1,0:T(8,128)(2,1)}, bf16[256,2048]{1,0:T(8,128)(2,1)}, u32[]{:S(2)}, u32[]{:S(2)}) collective-permute-start(bf16[256,2048]{1,0:T(8,128)(2,1)} %get-tuple-element.95), channel_id=1, source_target_pairs={{0,8},{4,12},{8,0},{12,4},{16,24},{20,28},{24,16},{28,20},{1,9},{5... | collective-permute-start | bytes 3145736 | tf_op jit(solution)/shard_map/ppermute | solution.py:239
  480.5 26.3 %collective-permute-start.21 = (bf16[256,2048]{1,0:T(8,128)(2,1)}, bf16[256,2048]{1,0:T(8,128)(2,1)}, u32[]{:S(2)}, u32[]{:S(2)}) collective-permute-start(bf16[256,2048]{1,0:T(8,128)(2,1)} %get-tuple-element.96), channel_id=1, source_target_pairs={{0,16},{4,20},{8,24},{12,28},{16,0},{20,4},{24,8},{28,12},{1,17},{... | collective-permute-start | bytes 3145736 | tf_op jit(solution)/shard_map/ppermute | solution.py:239
  489.8 36.5 %collective-permute-start.24 = (bf16[256,2048]{1,0:T(8,128)(2,1)}, bf16[256,2048]{1,0:T(8,128)(2,1)}, u32[]{:S(2)}, u32[]{:S(2)}) collective-permute-start(bf16[256,2048]{1,0:T(8,128)(2,1)} %get-tuple-element.93), channel_id=1, source_target_pairs={{0,8},{4,12},{8,0},{12,4},{16,24},{20,28},{24,16},{28,20},{1,9},{5... | collective-permute-start | bytes 3145736 | tf_op jit(solution)/shard_map/ppermute | solution.py:239
  498.1 31.2 %collective-permute-start.26 = (bf16[256,2048]{1,0:T(8,128)(2,1)}, bf16[256,2048]{1,0:T(8,128)(2,1)}, u32[]{:S(2)}, u32[]{:S(2)}) collective-permute-start(bf16[256,2048]{1,0:T(8,128)(2,1)} %get-tuple-element.94), channel_id=1, source_target_pairs={{0,16},{4,20},{8,24},{12,28},{16,0},{20,4},{24,8},{28,12},{1,17},{... | collective-permute-start | bytes 3145736 | tf_op jit(solution)/shard_map/ppermute | solution.py:239
  499.9 48.9 %collective-permute-start.29 = (bf16[2048,256]{0,1:T(8,128)(2,1)}, bf16[2048,256]{0,1:T(8,128)(2,1)S(1)}, u32[]{:S(2)}, u32[]{:S(2)}) collective-permute-start(bf16[2048,256]{0,1:T(8,128)(2,1)} %get-tuple-element.91), channel_id=1, source_target_pairs={{0,8},{4,12},{8,0},{12,4},{16,24},{20,28},{24,16},{28,20},{1,9},{5... | collective-permute-start | bytes 3145736 | tf_op jit(solution)/shard_map/ppermute | solution.py:239
  503.9 47.8 %collective-permute-start.31 = (bf16[2048,256]{0,1:T(8,128)(2,1)}, bf16[2048,256]{0,1:T(8,128)(2,1)S(1)}, u32[]{:S(2)}, u32[]{:S(2)}) collective-permute-start(bf16[2048,256]{0,1:T(8,128)(2,1)} %get-tuple-element.92), channel_id=1, source_target_pairs={{0,16},{4,20},{8,24},{12,28},{16,0},{20,4},{24,8},{28,12},{1,17},{... | collective-permute-start | bytes 3145736 | tf_op jit(solution)/shard_map/ppermute | solution.py:239
  509.4 50.6 %collective-permute-start.22 = (bf16[128,2048]{1,0:T(8,128)(2,1)S(1)}, bf16[128,2048]{1,0:T(8,128)(2,1)S(1)}, u32[]{:S(2)}, u32[]{:S(2)}) collective-permute-start(bf16[128,2048]{1,0:T(8,128)(2,1)S(1)} %slice.404), channel_id=1, source_target_pairs={{0,8},{4,12},{8,0},{12,4},{16,24},{20,28},{24,16},{28,20},{1,9},{5... | collective-permute-start | bytes 1572872 | tf_op jit(solution)/shard_map/ppermute | solution.py:239
  526.4 36.5 %collective-permute-start.20 = (bf16[128,2048]{1,0:T(8,128)(2,1)S(1)}, bf16[128,2048]{1,0:T(8,128)(2,1)S(1)}, u32[]{:S(2)}, u32[]{:S(2)}) collective-permute-start(bf16[128,2048]{1,0:T(8,128)(2,1)S(1)} %slice.405), channel_id=1, source_target_pairs={{0,16},{4,20},{8,24},{12,28},{16,0},{20,4},{24,8},{28,12},{1,17},{... | collective-permute-start | bytes 1572872 | tf_op jit(solution)/shard_map/ppermute | solution.py:239
  531.6 21.0 %copy-start.26 = (f32[256,2048]{1,0:T(8,128)}, f32[256,2048]{1,0:T(8,128)S(1)}, u32[]{:S(2)}) copy-start(f32[256,2048]{1,0:T(8,128)S(1)} %get-tuple-element.83) | copy-start | bytes 6291460
  531.6 21.0 %copy-start.28 = (f32[256,2048]{1,0:T(8,128)}, f32[256,2048]{1,0:T(8,128)S(1)}, u32[]{:S(2)}) copy-start(f32[256,2048]{1,0:T(8,128)S(1)} %get-tuple-element.84) | copy-start | bytes 6291460
  532.6 53.4 %collective-permute-start.27 = (bf16[128,2048]{1,0:T(8,128)(2,1)}, bf16[128,2048]{1,0:T(8,128)(2,1)S(1)}, u32[]{:S(2)}, u32[]{:S(2)}) collective-permute-start(bf16[128,2048]{1,0:T(8,128)(2,1)} %slice.402), channel_id=1, source_target_pairs={{0,8},{4,12},{8,0},{12,4},{16,24},{20,28},{24,16},{28,20},{1,9},{5... | collective-permute-start | bytes 1572872 | tf_op jit(solution)/shard_map/ppermute | solution.py:239
  548.7 38.8 %collective-permute-start.25 = (bf16[128,2048]{1,0:T(8,128)(2,1)}, bf16[128,2048]{1,0:T(8,128)(2,1)S(1)}, u32[]{:S(2)}, u32[]{:S(2)}) collective-permute-start(bf16[128,2048]{1,0:T(8,128)(2,1)} %slice.403), channel_id=1, source_target_pairs={{0,16},{4,20},{8,24},{12,28},{16,0},{20,4},{24,8},{28,12},{1,17},{... | collective-permute-start | bytes 1572872 | tf_op jit(solution)/shard_map/ppermute | solution.py:239
  552.6 26.8 %collective-permute-start.32 = (bf16[2048,128]{0,1:T(8,128)(2,1)S(1)}, bf16[2048,128]{0,1:T(8,128)(2,1)S(1)}, u32[]{:S(2)}, u32[]{:S(2)}) collective-permute-start(bf16[2048,128]{0,1:T(8,128)(2,1)S(1)} %slice.400), channel_id=1, source_target_pairs={{0,8},{4,12},{8,0},{12,4},{16,24},{20,28},{24,16},{28,20},{1,9},{5... | collective-permute-start | bytes 1572872 | tf_op jit(solution)/shard_map/ppermute | solution.py:239
  560.0 22.4 %collective-permute-start.30 = (bf16[2048,128]{0,1:T(8,128)(2,1)S(1)}, bf16[2048,128]{0,1:T(8,128)(2,1)S(1)}, u32[]{:S(2)}, u32[]{:S(2)}) collective-permute-start(bf16[2048,128]{0,1:T(8,128)(2,1)S(1)} %slice.401), channel_id=1, source_target_pairs={{0,16},{4,20},{8,24},{12,28},{16,0},{20,4},{24,8},{28,12},{1,17},{... | collective-permute-start | bytes 1572872 | tf_op jit(solution)/shard_map/ppermute | solution.py:239
  (39 other events, 150.4 us)
